TPU v7x, 32 devices: a whole 2x2x4 slice. The times are simulated.
32 devices in a mesh: data: 32 (over z, y, x, core).
Axes of the slice: x: 2, y: 2, z: 4, core: 2. Of those that a mesh axis runs over, the one named last changes fastest.
Arguments:
- feat_img: bfloat16 [16384, 2048], P('data')
- feat_txt: bfloat16 [16384, 512], P('data')
- w_img: bfloat16 [2048, 1024], replicated
- w_txt: bfloat16 [512, 1024], replicated
- log_temp: float32 [], replicated
- logit_bias: float32 [], replicated
- pair_ids: int32 [16384], P('data')
Outputs:
- output 1: float32 [], replicated
- output 2: float32 [], replicated
- output 3: float32 [], replicated
- output 4: float32 [2048, 1024], replicated
- output 5: float32 [512, 1024], replicated
All inputs are finite; a program needn't handle non-finite values.
Results may differ from a plain program's by a relative error of at most 0.001.
Values are sent between devices in bfloat16 or wider.
A program may use at most 1 GiB of HBM per device.

v0:
```python
import jax
import jax.numpy as jnp
from jax import lax
from jax.sharding import PartitionSpec as P

CONTRACT_ROWS = (((0,), (0,)), ((), ()))
CONTRACT_COLS = (((1,), (1,)), ((), ()))


def embed_rows(feat_rows, weights):
    raw_emb = jnp.dot(feat_rows, weights, preferred_element_type=jnp.float32)
    inv_norm = lax.rsqrt(jnp.sum(raw_emb * raw_emb, axis=1, keepdims=True))
    unit_emb = raw_emb * inv_norm
    return unit_emb, inv_norm, unit_emb.astype(jnp.bfloat16)


def weight_grad(feat_rows, unit_emb, inv_norm, grad_emb):
    raw_grad = inv_norm * (grad_emb - unit_emb * jnp.sum(unit_emb * grad_emb, axis=1, keepdims=True))
    return lax.dot_general(feat_rows, raw_grad.astype(jnp.bfloat16), CONTRACT_ROWS, preferred_element_type=jnp.float32)


def tile_terms(emb_img, ids_img, emb_txt, ids_txt, temp_scale, logit_bias, total_rows):
    sim_tile = lax.dot_general(emb_img, emb_txt, CONTRACT_COLS, preferred_element_type=jnp.float32)
    label_sign = jnp.where(ids_img[:, None] == ids_txt[None, :], 1.0, -1.0).astype(jnp.float32)
    margin = -label_sign * (temp_scale * sim_tile + logit_bias)
    grad_tile = -label_sign * jax.nn.sigmoid(margin) / total_rows
    grad_bf = grad_tile.astype(jnp.bfloat16)
    part_img = jnp.dot(grad_bf, emb_txt, preferred_element_type=jnp.float32)
    part_txt = lax.dot_general(grad_bf, emb_img, CONTRACT_ROWS, preferred_element_type=jnp.float32)
    loss_part = jnp.sum(jax.nn.softplus(margin))
    return part_img, part_txt, loss_part, jnp.sum(grad_tile * sim_tile), jnp.sum(grad_tile)


def solution(mesh):
    n_dev = mesh.shape["data"]
    next_perm = [(src_dev, (src_dev + 1) % n_dev) for src_dev in range(n_dev)]

    def local_fn(feat_img, feat_txt, w_img, w_txt, log_temp, logit_bias, pair_ids):
        total_rows = feat_img.shape[0] * n_dev
        temp_scale = jnp.exp(log_temp)
        unit_img, inv_img, emb_img = embed_rows(feat_img, w_img)
        unit_txt, inv_txt, emb_txt = embed_rows(feat_txt, w_txt)

        def visit_block(hop_index, loop_state):
            txt_blk, ids_blk, acc_txt, acc_img, loss_sum, temp_sum, bias_sum = loop_state
            part_img, part_txt, loss_part, temp_part, bias_part = tile_terms(
                emb_img, pair_ids, txt_blk, ids_blk, temp_scale, logit_bias, total_rows)
            txt_blk, ids_blk, acc_txt = lax.ppermute((txt_blk, ids_blk, acc_txt + part_txt), "data", next_perm)
            return (txt_blk, ids_blk, acc_txt, acc_img + part_img,
                    loss_sum + loss_part, temp_sum + temp_part, bias_sum + bias_part)

        zero_rows = jnp.zeros(emb_img.shape, jnp.float32)
        zero_sum = jnp.zeros((), jnp.float32)
        loop_state = (emb_txt, pair_ids, zero_rows, zero_rows, zero_sum, zero_sum, zero_sum)
        loop_state = lax.fori_loop(0, n_dev - 1, visit_block, loop_state)
        txt_blk, ids_blk, acc_txt, acc_img, loss_sum, temp_sum, bias_sum = loop_state
        part_img, part_txt, loss_part, temp_part, bias_part = tile_terms(
            emb_img, pair_ids, txt_blk, ids_blk, temp_scale, logit_bias, total_rows)
        home_txt = lax.ppermute(acc_txt + part_txt, "data", next_perm)
        grad_img = temp_scale * (acc_img + part_img)
        grad_txt = temp_scale * home_txt
        dw_img = weight_grad(feat_img, unit_img, inv_img, grad_img)
        dw_txt = weight_grad(feat_txt, unit_txt, inv_txt, grad_txt)
        totals = lax.psum((loss_sum + loss_part, temp_sum + temp_part, bias_sum + bias_part, dw_img, dw_txt), "data")
        return totals[0] / total_rows, temp_scale * totals[1], totals[2], totals[3], totals[4]

    return jax.shard_map(
        local_fn,
        mesh=mesh,
        in_specs=(P("data", None), P("data", None), P(None, None), P(None, None), P(), P(), P("data")),
        out_specs=(P(), P(), P(), P(None, None), P(None, None)),
        check_vma=False,
    )
```

profile of v0, /device:TPU:0, one launch (start us, length us, event | category | flops | bytes accessed | tf_op | source)
XLA Modules:
  0.0 1858.5 jit_solution(6408386214913583736)
XLA Ops:
  18.2 1580.7 %while.23 = (s32[]{:T(128)}, bf16[512,1024]{1,0:T(8,128)(2,1)S(1)}, s32[512]{0:T(512)S(1)}, f32[512,1024]{1,0:T(8,128)}, f32[512,1024]{1,0:T(8,128)}, /*index=5*...) while((s32[]{:T(128)}, bf16[512,1024]{1,0:T(8,128)(2,1)S(1)}, ...), condition=%wide.region_6.7_spmd.clone, body=%wide.region_2.6_spmd.clone.sunk | while | flops 1623982080 | bytes 38822276 | solution.py:55
  139.1 33.1 %collective-permute-done.1 = s32[512]{0:T(512)S(1)} collective-permute-done((s32[512]{0:T(512)S(1)}, s32[512]{0:T(512)S(1)}, u32[]{:S(2)}, u32[]{:S(2)}) %collective-permute-start.1) | collective-permute-done | bytes 2080 | tf_op jit(solution)/shard_map/while/body/eval_jaxpr/ppermute | solution.py:48
  190.1 33.1 %collective-permute-done.1 = s32[512]{0:T(512)S(1)} collective-permute-done((s32[512]{0:T(512)S(1)}, s32[512]{0:T(512)S(1)}, u32[]{:S(2)}, u32[]{:S(2)}) %collective-permute-start.1) | collective-permute-done | bytes 2080 | tf_op jit(solution)/shard_map/while/body/eval_jaxpr/ppermute | solution.py:48
  241.0 33.1 %collective-permute-done.1 = s32[512]{0:T(512)S(1)} collective-permute-done((s32[512]{0:T(512)S(1)}, s32[512]{0:T(512)S(1)}, u32[]{:S(2)}, u32[]{:S(2)}) %collective-permute-start.1) | collective-permute-done | bytes 2080 | tf_op jit(solution)/shard_map/while/body/eval_jaxpr/ppermute | solution.py:48
  292.0 33.1 %collective-permute-done.1 = s32[512]{0:T(512)S(1)} collective-permute-done((s32[512]{0:T(512)S(1)}, s32[512]{0:T(512)S(1)}, u32[]{:S(2)}, u32[]{:S(2)}) %collective-permute-start.1) | collective-permute-done | bytes 2080 | tf_op jit(solution)/shard_map/while/body/eval_jaxpr/ppermute | solution.py:48
  342.9 33.1 %collective-permute-done.1 = s32[512]{0:T(512)S(1)} collective-permute-done((s32[512]{0:T(512)S(1)}, s32[512]{0:T(512)S(1)}, u32[]{:S(2)}, u32[]{:S(2)}) %collective-permute-start.1) | collective-permute-done | bytes 2080 | tf_op jit(solution)/shard_map/while/body/eval_jaxpr/ppermute | solution.py:48
  393.9 33.1 %collective-permute-done.1 = s32[512]{0:T(512)S(1)} collective-permute-done((s32[512]{0:T(512)S(1)}, s32[512]{0:T(512)S(1)}, u32[]{:S(2)}, u32[]{:S(2)}) %collective-permute-start.1) | collective-permute-done | bytes 2080 | tf_op jit(solution)/shard_map/while/body/eval_jaxpr/ppermute | solution.py:48
  444.8 33.1 %collective-permute-done.1 = s32[512]{0:T(512)S(1)} collective-permute-done((s32[512]{0:T(512)S(1)}, s32[512]{0:T(512)S(1)}, u32[]{:S(2)}, u32[]{:S(2)}) %collective-permute-start.1) | collective-permute-done | bytes 2080 | tf_op jit(solution)/shard_map/while/body/eval_jaxpr/ppermute | solution.py:48
  495.8 33.1 %collective-permute-done.1 = s32[512]{0:T(512)S(1)} collective-permute-done((s32[512]{0:T(512)S(1)}, s32[512]{0:T(512)S(1)}, u32[]{:S(2)}, u32[]{:S(2)}) %collective-permute-start.1) | collective-permute-done | bytes 2080 | tf_op jit(solution)/shard_map/while/body/eval_jaxpr/ppermute | solution.py:48
  546.7 33.1 %collective-permute-done.1 = s32[512]{0:T(512)S(1)} collective-permute-done((s32[512]{0:T(512)S(1)}, s32[512]{0:T(512)S(1)}, u32[]{:S(2)}, u32[]{:S(2)}) %collective-permute-start.1) | collective-permute-done | bytes 2080 | tf_op jit(solution)/shard_map/while/body/eval_jaxpr/ppermute | solution.py:48
  597.7 33.1 %collective-permute-done.1 = s32[512]{0:T(512)S(1)} collective-permute-done((s32[512]{0:T(512)S(1)}, s32[512]{0:T(512)S(1)}, u32[]{:S(2)}, u32[]{:S(2)}) %collective-permute-start.1) | collective-permute-done | bytes 2080 | tf_op jit(solution)/shard_map/while/body/eval_jaxpr/ppermute | solution.py:48
  648.7 33.1 %collective-permute-done.1 = s32[512]{0:T(512)S(1)} collective-permute-done((s32[512]{0:T(512)S(1)}, s32[512]{0:T(512)S(1)}, u32[]{:S(2)}, u32[]{:S(2)}) %collective-permute-start.1) | collective-permute-done | bytes 2080 | tf_op jit(solution)/shard_map/while/body/eval_jaxpr/ppermute | solution.py:48
  699.6 33.1 %collective-permute-done.1 = s32[512]{0:T(512)S(1)} collective-permute-done((s32[512]{0:T(512)S(1)}, s32[512]{0:T(512)S(1)}, u32[]{:S(2)}, u32[]{:S(2)}) %collective-permute-start.1) | collective-permute-done | bytes 2080 | tf_op jit(solution)/shard_map/while/body/eval_jaxpr/ppermute | solution.py:48
  750.6 33.1 %collective-permute-done.1 = s32[512]{0:T(512)S(1)} collective-permute-done((s32[512]{0:T(512)S(1)}, s32[512]{0:T(512)S(1)}, u32[]{:S(2)}, u32[]{:S(2)}) %collective-permute-start.1) | collective-permute-done | bytes 2080 | tf_op jit(solution)/shard_map/while/body/eval_jaxpr/ppermute | solution.py:48
  852.5 33.1 %collective-permute-done.1 = s32[512]{0:T(512)S(1)} collective-permute-done((s32[512]{0:T(512)S(1)}, s32[512]{0:T(512)S(1)}, u32[]{:S(2)}, u32[]{:S(2)}) %collective-permute-start.1) | collective-permute-done | bytes 2080 | tf_op jit(solution)/shard_map/while/body/eval_jaxpr/ppermute | solution.py:48
  954.4 33.1 %collective-permute-done.1 = s32[512]{0:T(512)S(1)} collective-permute-done((s32[512]{0:T(512)S(1)}, s32[512]{0:T(512)S(1)}, u32[]{:S(2)}, u32[]{:S(2)}) %collective-permute-start.1) | collective-permute-done | bytes 2080 | tf_op jit(solution)/shard_map/while/body/eval_jaxpr/ppermute | solution.py:48
  1056.3 33.1 %collective-permute-done.1 = s32[512]{0:T(512)S(1)} collective-permute-done((s32[512]{0:T(512)S(1)}, s32[512]{0:T(512)S(1)}, u32[]{:S(2)}, u32[]{:S(2)}) %collective-permute-start.1) | collective-permute-done | bytes 2080 | tf_op jit(solution)/shard_map/while/body/eval_jaxpr/ppermute | solution.py:48
  1158.2 33.1 %collective-permute-done.1 = s32[512]{0:T(512)S(1)} collective-permute-done((s32[512]{0:T(512)S(1)}, s32[512]{0:T(512)S(1)}, u32[]{:S(2)}, u32[]{:S(2)}) %collective-permute-start.1) | collective-permute-done | bytes 2080 | tf_op jit(solution)/shard_map/while/body/eval_jaxpr/ppermute | solution.py:48
  1260.1 33.1 %collective-permute-done.1 = s32[512]{0:T(512)S(1)} collective-permute-done((s32[512]{0:T(512)S(1)}, s32[512]{0:T(512)S(1)}, u32[]{:S(2)}, u32[]{:S(2)}) %collective-permute-start.1) | collective-permute-done | bytes 2080 | tf_op jit(solution)/shard_map/while/body/eval_jaxpr/ppermute | solution.py:48
  1362.0 33.1 %collective-permute-done.1 = s32[512]{0:T(512)S(1)} collective-permute-done((s32[512]{0:T(512)S(1)}, s32[512]{0:T(512)S(1)}, u32[]{:S(2)}, u32[]{:S(2)}) %collective-permute-start.1) | collective-permute-done | bytes 2080 | tf_op jit(solution)/shard_map/while/body/eval_jaxpr/ppermute | solution.py:48
  1463.9 33.1 %collective-permute-done.1 = s32[512]{0:T(512)S(1)} collective-permute-done((s32[512]{0:T(512)S(1)}, s32[512]{0:T(512)S(1)}, u32[]{:S(2)}, u32[]{:S(2)}) %collective-permute-start.1) | collective-permute-done | bytes 2080 | tf_op jit(solution)/shard_map/while/body/eval_jaxpr/ppermute | solution.py:48
  1565.9 33.1 %collective-permute-done.1 = s32[512]{0:T(512)S(1)} collective-permute-done((s32[512]{0:T(512)S(1)}, s32[512]{0:T(512)S(1)}, u32[]{:S(2)}, u32[]{:S(2)}) %collective-permute-start.1) | collective-permute-done | bytes 2080 | tf_op jit(solution)/shard_map/while/body/eval_jaxpr/ppermute | solution.py:48
  1639.7 38.1 %all-reduce = (f32[]{:T(128)}, f32[]{:T(128)}, f32[]{:T(128)}) all-reduce(f32[]{:T(128)S(6)} %add.71, f32[]{:T(128)S(6)} %add.73, f32[]{:T(128)S(6)} %add.74), channel_id=1, replica_groups=mesh['data'=32] {'data'}, use_global_device_ids=true, to_apply=%region_8.9 | all-reduce | flops 3 | bytes 24 | tf_op jit(solution)/shard_map/psum | solution.py:64
  1679.1 158.2 %all-reduce.4.cloned.1.call-done = (f32[2048,1024]{0,1:T(8,128)}, f32[512,1024]{0,1:T(8,128)}) async-done(((f32[2048,1024]{0,1:T(8,128)}, f32[512,1024]{0,1:T(8,128)}), (f32[2048,1024]{0,1:T(8,128)}, f32[512,1024]{0,1:T(8,128)})) %all-reduce.4.cloned.1.call-update) | async-done | bytes 10485776 | tf_op jit(solution)/shard_map/psum | solution.py:64
  (486 shorter events, 884.8 us)
Async XLA Ops:
  7.2 1830.1 %all-reduce.4.cloned.1.call-start = ((), (), s32[]{:S(2)}) async-start(), calls=%async_computation | async-start | bytes 20971520 | tf_op jit(solution)/shard_map/psum | solution.py:64
  28.9 41.4 %collective-permute-start.2 = (f32[512,1024]{1,0:T(8,128)}, f32[512,1024]{1,0:T(8,128)}, u32[]{:S(2)}, u32[]{:S(2)}) collective-permute-start(f32[512,1024]{1,0:T(8,128)} %convolution_add_fusion.3), channel_id=1, source_target_pairs={{0,1},{1,2},{2,3},{3,4},{4,5},{5,6},{6,7},{7,8},{8,9},{9,10},{10,1... | collective-permute-start | bytes 6291464 | tf_op jit(solution)/shard_map/while/body/eval_jaxpr/ppermute | solution.py:48
  29.4 40.9 %collective-permute-start = (bf16[512,1024]{1,0:T(8,128)(2,1)}, bf16[512,1024]{1,0:T(8,128)(2,1)S(1)}, u32[]{:S(2)}, u32[]{:S(2)}) collective-permute-start(bf16[512,1024]{1,0:T(8,128)(2,1)} %copy.23), channel_id=1, source_target_pairs={{0,1},{1,2},{2,3},{3,4},{4,5},{5,6},{6,7},{7,8},{8,9},{9,10},{10,1... | collective-permute-start | bytes 3145736 | tf_op jit(solution)/shard_map/while/body/eval_jaxpr/ppermute | solution.py:48
  80.9 40.3 %collective-permute-start.2 = (f32[512,1024]{1,0:T(8,128)}, f32[512,1024]{1,0:T(8,128)}, u32[]{:S(2)}, u32[]{:S(2)}) collective-permute-start(f32[512,1024]{1,0:T(8,128)} %convolution_add_fusion.3), channel_id=1, source_target_pairs={{0,1},{1,2},{2,3},{3,4},{4,5},{5,6},{6,7},{7,8},{8,9},{9,10},{10,1... | collective-permute-start | bytes 6291464 | tf_op jit(solution)/shard_map/while/body/eval_jaxpr/ppermute | solution.py:48
  131.9 40.3 %collective-permute-start.2 = (f32[512,1024]{1,0:T(8,128)}, f32[512,1024]{1,0:T(8,128)}, u32[]{:S(2)}, u32[]{:S(2)}) collective-permute-start(f32[512,1024]{1,0:T(8,128)} %convolution_add_fusion.3), channel_id=1, source_target_pairs={{0,1},{1,2},{2,3},{3,4},{4,5},{5,6},{6,7},{7,8},{8,9},{9,10},{10,1... | collective-permute-start | bytes 6291464 | tf_op jit(solution)/shard_map/while/body/eval_jaxpr/ppermute | solution.py:48
  233.8 40.3 %collective-permute-start.2 = (f32[512,1024]{1,0:T(8,128)}, f32[512,1024]{1,0:T(8,128)}, u32[]{:S(2)}, u32[]{:S(2)}) collective-permute-start(f32[512,1024]{1,0:T(8,128)} %convolution_add_fusion.3), channel_id=1, source_target_pairs={{0,1},{1,2},{2,3},{3,4},{4,5},{5,6},{6,7},{7,8},{8,9},{9,10},{10,1... | collective-permute-start | bytes 6291464 | tf_op jit(solution)/shard_map/while/body/eval_jaxpr/ppermute | solution.py:48
  284.7 40.3 %collective-permute-start.2 = (f32[512,1024]{1,0:T(8,128)}, f32[512,1024]{1,0:T(8,128)}, u32[]{:S(2)}, u32[]{:S(2)}) collective-permute-start(f32[512,1024]{1,0:T(8,128)} %convolution_add_fusion.3), channel_id=1, source_target_pairs={{0,1},{1,2},{2,3},{3,4},{4,5},{5,6},{6,7},{7,8},{8,9},{9,10},{10,1... | collective-permute-start | bytes 6291464 | tf_op jit(solution)/shard_map/while/body/eval_jaxpr/ppermute | solution.py:48
  335.7 40.3 %collective-permute-start.2 = (f32[512,1024]{1,0:T(8,128)}, f32[512,1024]{1,0:T(8,128)}, u32[]{:S(2)}, u32[]{:S(2)}) collective-permute-start(f32[512,1024]{1,0:T(8,128)} %convolution_add_fusion.3), channel_id=1, source_target_pairs={{0,1},{1,2},{2,3},{3,4},{4,5},{5,6},{6,7},{7,8},{8,9},{9,10},{10,1... | collective-permute-start | bytes 6291464 | tf_op jit(solution)/shard_map/while/body/eval_jaxpr/ppermute | solution.py:48
  386.7 40.3 %collective-permute-start.2 = (f32[512,1024]{1,0:T(8,128)}, f32[512,1024]{1,0:T(8,128)}, u32[]{:S(2)}, u32[]{:S(2)}) collective-permute-start(f32[512,1024]{1,0:T(8,128)} %convolution_add_fusion.3), channel_id=1, source_target_pairs={{0,1},{1,2},{2,3},{3,4},{4,5},{5,6},{6,7},{7,8},{8,9},{9,10},{10,1... | collective-permute-start | bytes 6291464 | tf_op jit(solution)/shard_map/while/body/eval_jaxpr/ppermute | solution.py:48
  437.6 40.3 %collective-permute-start.2 = (f32[512,1024]{1,0:T(8,128)}, f32[512,1024]{1,0:T(8,128)}, u32[]{:S(2)}, u32[]{:S(2)}) collective-permute-start(f32[512,1024]{1,0:T(8,128)} %convolution_add_fusion.3), channel_id=1, source_target_pairs={{0,1},{1,2},{2,3},{3,4},{4,5},{5,6},{6,7},{7,8},{8,9},{9,10},{10,1... | collective-permute-start | bytes 6291464 | tf_op jit(solution)/shard_map/while/body/eval_jaxpr/ppermute | solution.py:48
  488.6 40.3 %collective-permute-start.2 = (f32[512,1024]{1,0:T(8,128)}, f32[512,1024]{1,0:T(8,128)}, u32[]{:S(2)}, u32[]{:S(2)}) collective-permute-start(f32[512,1024]{1,0:T(8,128)} %convolution_add_fusion.3), channel_id=1, source_target_pairs={{0,1},{1,2},{2,3},{3,4},{4,5},{5,6},{6,7},{7,8},{8,9},{9,10},{10,1... | collective-permute-start | bytes 6291464 | tf_op jit(solution)/shard_map/while/body/eval_jaxpr/ppermute | solution.py:48
  539.5 40.3 %collective-permute-start.2 = (f32[512,1024]{1,0:T(8,128)}, f32[512,1024]{1,0:T(8,128)}, u32[]{:S(2)}, u32[]{:S(2)}) collective-permute-start(f32[512,1024]{1,0:T(8,128)} %convolution_add_fusion.3), channel_id=1, source_target_pairs={{0,1},{1,2},{2,3},{3,4},{4,5},{5,6},{6,7},{7,8},{8,9},{9,10},{10,1... | collective-permute-start | bytes 6291464 | tf_op jit(solution)/shard_map/while/body/eval_jaxpr/ppermute | solution.py:48
  590.5 40.3 %collective-permute-start.2 = (f32[512,1024]{1,0:T(8,128)}, f32[512,1024]{1,0:T(8,128)}, u32[]{:S(2)}, u32[]{:S(2)}) collective-permute-start(f32[512,1024]{1,0:T(8,128)} %convolution_add_fusion.3), channel_id=1, source_target_pairs={{0,1},{1,2},{2,3},{3,4},{4,5},{5,6},{6,7},{7,8},{8,9},{9,10},{10,1... | collective-permute-start | bytes 6291464 | tf_op jit(solution)/shard_map/while/body/eval_jaxpr/ppermute | solution.py:48
  641.4 40.3 %collective-permute-start.2 = (f32[512,1024]{1,0:T(8,128)}, f32[512,1024]{1,0:T(8,128)}, u32[]{:S(2)}, u32[]{:S(2)}) collective-permute-start(f32[512,1024]{1,0:T(8,128)} %convolution_add_fusion.3), channel_id=1, source_target_pairs={{0,1},{1,2},{2,3},{3,4},{4,5},{5,6},{6,7},{7,8},{8,9},{9,10},{10,1... | collective-permute-start | bytes 6291464 | tf_op jit(solution)/shard_map/while/body/eval_jaxpr/ppermute | solution.py:48
  692.4 40.3 %collective-permute-start.2 = (f32[512,1024]{1,0:T(8,128)}, f32[512,1024]{1,0:T(8,128)}, u32[]{:S(2)}, u32[]{:S(2)}) collective-permute-start(f32[512,1024]{1,0:T(8,128)} %convolution_add_fusion.3), channel_id=1, source_target_pairs={{0,1},{1,2},{2,3},{3,4},{4,5},{5,6},{6,7},{7,8},{8,9},{9,10},{10,1... | collective-permute-start | bytes 6291464 | tf_op jit(solution)/shard_map/while/body/eval_jaxpr/ppermute | solution.py:48
  743.3 40.3 %collective-permute-start.2 = (f32[512,1024]{1,0:T(8,128)}, f32[512,1024]{1,0:T(8,128)}, u32[]{:S(2)}, u32[]{:S(2)}) collective-permute-start(f32[512,1024]{1,0:T(8,128)} %convolution_add_fusion.3), channel_id=1, source_target_pairs={{0,1},{1,2},{2,3},{3,4},{4,5},{5,6},{6,7},{7,8},{8,9},{9,10},{10,1... | collective-permute-start | bytes 6291464 | tf_op jit(solution)/shard_map/while/body/eval_jaxpr/ppermute | solution.py:48
  794.3 40.3 %collective-permute-start.2 = (f32[512,1024]{1,0:T(8,128)}, f32[512,1024]{1,0:T(8,128)}, u32[]{:S(2)}, u32[]{:S(2)}) collective-permute-start(f32[512,1024]{1,0:T(8,128)} %convolution_add_fusion.3), channel_id=1, source_target_pairs={{0,1},{1,2},{2,3},{3,4},{4,5},{5,6},{6,7},{7,8},{8,9},{9,10},{10,1... | collective-permute-start | bytes 6291464 | tf_op jit(solution)/shard_map/while/body/eval_jaxpr/ppermute | solution.py:48
  845.3 40.3 %collective-permute-start.2 = (f32[512,1024]{1,0:T(8,128)}, f32[512,1024]{1,0:T(8,128)}, u32[]{:S(2)}, u32[]{:S(2)}) collective-permute-start(f32[512,1024]{1,0:T(8,128)} %convolution_add_fusion.3), channel_id=1, source_target_pairs={{0,1},{1,2},{2,3},{3,4},{4,5},{5,6},{6,7},{7,8},{8,9},{9,10},{10,1... | collective-permute-start | bytes 6291464 | tf_op jit(solution)/shard_map/while/body/eval_jaxpr/ppermute | solution.py:48
  896.2 40.3 %collective-permute-start.2 = (f32[512,1024]{1,0:T(8,128)}, f32[512,1024]{1,0:T(8,128)}, u32[]{:S(2)}, u32[]{:S(2)}) collective-permute-start(f32[512,1024]{1,0:T(8,128)} %convolution_add_fusion.3), channel_id=1, source_target_pairs={{0,1},{1,2},{2,3},{3,4},{4,5},{5,6},{6,7},{7,8},{8,9},{9,10},{10,1... | collective-permute-start | bytes 6291464 | tf_op jit(solution)/shard_map/while/body/eval_jaxpr/ppermute | solution.py:48
  947.2 40.3 %collective-permute-start.2 = (f32[512,1024]{1,0:T(8,128)}, f32[512,1024]{1,0:T(8,128)}, u32[]{:S(2)}, u32[]{:S(2)}) collective-permute-start(f32[512,1024]{1,0:T(8,128)} %convolution_add_fusion.3), channel_id=1, source_target_pairs={{0,1},{1,2},{2,3},{3,4},{4,5},{5,6},{6,7},{7,8},{8,9},{9,10},{10,1... | collective-permute-start | bytes 6291464 | tf_op jit(solution)/shard_map/while/body/eval_jaxpr/ppermute | solution.py:48
  998.1 40.3 %collective-permute-start.2 = (f32[512,1024]{1,0:T(8,128)}, f32[512,1024]{1,0:T(8,128)}, u32[]{:S(2)}, u32[]{:S(2)}) collective-permute-start(f32[512,1024]{1,0:T(8,128)} %convolution_add_fusion.3), channel_id=1, source_target_pairs={{0,1},{1,2},{2,3},{3,4},{4,5},{5,6},{6,7},{7,8},{8,9},{9,10},{10,1... | collective-permute-start | bytes 6291464 | tf_op jit(solution)/shard_map/while/body/eval_jaxpr/ppermute | solution.py:48
  1049.1 40.3 %collective-permute-start.2 = (f32[512,1024]{1,0:T(8,128)}, f32[512,1024]{1,0:T(8,128)}, u32[]{:S(2)}, u32[]{:S(2)}) collective-permute-start(f32[512,1024]{1,0:T(8,128)} %convolution_add_fusion.3), channel_id=1, source_target_pairs={{0,1},{1,2},{2,3},{3,4},{4,5},{5,6},{6,7},{7,8},{8,9},{9,10},{10,1... | collective-permute-start | bytes 6291464 | tf_op jit(solution)/shard_map/while/body/eval_jaxpr/ppermute | solution.py:48
  1100.0 40.3 %collective-permute-start.2 = (f32[512,1024]{1,0:T(8,128)}, f32[512,1024]{1,0:T(8,128)}, u32[]{:S(2)}, u32[]{:S(2)}) collective-permute-start(f32[512,1024]{1,0:T(8,128)} %convolution_add_fusion.3), channel_id=1, source_target_pairs={{0,1},{1,2},{2,3},{3,4},{4,5},{5,6},{6,7},{7,8},{8,9},{9,10},{10,1... | collective-permute-start | bytes 6291464 | tf_op jit(solution)/shard_map/while/body/eval_jaxpr/ppermute | solution.py:48
  1151.0 40.3 %collective-permute-start.2 = (f32[512,1024]{1,0:T(8,128)}, f32[512,1024]{1,0:T(8,128)}, u32[]{:S(2)}, u32[]{:S(2)}) collective-permute-start(f32[512,1024]{1,0:T(8,128)} %convolution_add_fusion.3), channel_id=1, source_target_pairs={{0,1},{1,2},{2,3},{3,4},{4,5},{5,6},{6,7},{7,8},{8,9},{9,10},{10,1... | collective-permute-start | bytes 6291464 | tf_op jit(solution)/shard_map/while/body/eval_jaxpr/ppermute | solution.py:48
  (144 other events, 3120.7 us)
Sparse Core Ops, SparseCore 0:
  1637.9 199.3 all-reduce.3
where the time goes:
time: 1870 us; the launch traced here: 1860 us
  waiting for transfers between devices  1200 us (64%)
  matrix products  462 us (25%)
  local copies, waits for them, and re-layouts  64.1 us (3%)
  loops' own time  61.3 us (3%)
  blocking collectives  38.1 us (2%)
  between operations  21.1 us (1%)
    ppermute x93, waiting for transfers between devices, visit_block(): lax.ppermute((txt_blk, ids_blk, acc_txt + part_txt), 'data', next_perm)  1020 us
    dot_general x32, matrix products, tile_terms(): part_img = jnp.dot(grad_bf, emb_txt, preferred_element_type=jnp.float32)  161 us
    psum x1, waiting for transfers between devices, local_fn(): lax.psum((loss_sum + loss_part, temp_sum + temp_part, bias_sum + bias_par...  158 us
    dot_general x32, matrix products, tile_terms(): lax.dot_general(grad_bf, emb_img, CONTRACT_ROWS, preferred_element_type=j...  147 us
    dot_general x32, matrix products, tile_terms(): lax.dot_general(emb_img, emb_txt, CONTRACT_COLS, preferred_element_type=j...  139 us
    another operation x1, loops' own time, local_fn(): loop_state = lax.fori_loop(0, n_dev - 1, visit_block, loop_state)  61.3 us
    while x186, local copies, waits for them, and re-layouts  49.5 us
    psum x1, blocking collectives, local_fn(): lax.psum((loss_sum + loss_part, temp_sum + temp_part, bias_sum + bias_par...  38.1 us
  transfers between devices with their start and end apart: 95, of which 33 were waited for; matrix products, arithmetic and copies ran while one was open for 9% of the time, Pallas kernels for 0%

commit v1 on v0

v1 whole, which is shorter than its diff:
```python
import functools

import jax
import jax.numpy as jnp
from jax import lax
from jax.experimental import pallas as pl
from jax.experimental.pallas import tpu as pltpu
from jax.sharding import PartitionSpec as P

CONTRACT_ROWS = (((0,), (0,)), ((), ()))
CONTRACT_COLS = (((1,), (1,)), ((), ()))
LOG2E = 1.4426950408889634
LN2 = 0.6931471805599453
ROW_CHUNK = 256
COL_CHUNK = 256


def embed_rows(feat_rows, weights):
    raw_emb = jnp.dot(feat_rows, weights, preferred_element_type=jnp.float32)
    inv_norm = lax.rsqrt(jnp.sum(raw_emb * raw_emb, axis=1, keepdims=True))
    unit_emb = raw_emb * inv_norm
    return unit_emb, inv_norm, unit_emb.astype(jnp.bfloat16)


def weight_grad(feat_rows, unit_emb, inv_norm, grad_emb):
    raw_grad = inv_norm * (grad_emb - unit_emb * jnp.sum(unit_emb * grad_emb, axis=1, keepdims=True))
    return lax.dot_general(feat_rows, raw_grad.astype(jnp.bfloat16), CONTRACT_ROWS, preferred_element_type=jnp.float32)


def log1p_sum(expo):
    terms = [expo[8 * k:8 * k + 8] for k in range(expo.shape[0] // 8)]
    while len(terms) > 1:
        terms = [terms[2 * k] + terms[2 * k + 1] + terms[2 * k] * terms[2 * k + 1] for k in range(len(terms) // 2)]
    prod = terms[0]
    one_plus = 1.0 + prod
    return jnp.log(one_plus) + (prod - (one_plus - 1.0)) / one_plus


def fold_rows(tile):
    terms = [tile[8 * k:8 * k + 8] for k in range(tile.shape[0] // 8)]
    while len(terms) > 1:
        terms = [terms[2 * k] + terms[2 * k + 1] for k in range(len(terms) // 2)]
    return terms[0]


AXES = {"c": (2, 1), "x": (2, 2), "y": (2, 4), "z": (4, 8)}
MESH_ID = pl.DeviceIdType.MESH


def coordinate(me, axis):
    size, stride = AXES[axis]
    return lax.rem(lax.div(me, stride), size)


def peer_of(me, axis, dist):
    size, stride = AXES[axis]
    here = coordinate(me, axis)
    return me + (lax.rem(here + dist, size) - here) * stride


def rows_at(start, size):
    return pl.ds(pl.multiple_of(start, 8), size)


class Slab:
    def __init__(self, src, dst, row0, rows, order):
        self.src, self.dst, self.row0, self.rows, self.order = src, dst, row0, rows, order

    def piece(self, stage):
        rows = self.rows
        for axis in self.order[:stage + 1]:
            rows //= AXES[axis][0]
        return rows


def sum_plan(wi_rows, wt_rows, sub):
    plan = []
    for k in range(sub):
        half = wi_rows // 2 // sub
        part = wt_rows // sub
        plan.append((0, k * half, half, "cxyz"))
        plan.append((0, wi_rows // 2 + k * half, half, "cyxz"))
        plan.append((1, k * part, part, "czxy"))
    plan.append((2, 0, 256, "cxyz"))
    return plan


def sum_kernel(plan, *refs):
    ins, outs = refs[:3], refs[3:6]
    n = len(plan)
    held = refs[6:6 + n]
    land = refs[6 + n:6 + 5 * n]
    send_sem, recv_sem = refs[6 + 5 * n:]
    me = lax.axis_index("data")
    slabs = [Slab(ins[a], outs[a], row0, rows, order) for a, row0, rows, order in plan]

    barrier = pltpu.get_barrier_semaphore()
    partners = [peer_of(me, axis, d) for axis in "cxyz" for d in range(1, AXES[axis][0])]
    for dev in partners:
        pl.semaphore_signal(barrier, inc=1, device_id=(dev,), device_id_type=MESH_ID)
    pl.semaphore_wait(barrier, len(partners))

    counter = [0]
    started = []

    def send(src, dst, dev):
        k = counter[0]
        counter[0] += 1
        copy = pltpu.make_async_remote_copy(
            src_ref=src, dst_ref=dst, send_sem=send_sem.at[k], recv_sem=recv_sem.at[k],
            device_id=(dev,), device_id_type=MESH_ID)
        copy.start()
        started.append(copy)
        return copy

    offs = [0] * n
    pending = [None] * n

    def scatter(i, stage):
        slab = slabs[i]
        axis = slab.order[stage]
        size = AXES[axis][0]
        piece = slab.piece(stage)
        here = coordinate(me, axis)
        copies = []
        for d in range(1, size):
            there = lax.rem(here + d, size)
            if stage == 0:
                src = slab.src.at[rows_at(slab.row0 + there * piece, piece)]
            else:
                src = held[i].at[rows_at(offs[i] + there * piece, piece)]
            copies.append(send(src, land[4 * i + stage].at[d - 1], peer_of(me, axis, d)))
        pending[i] = copies

    def absorb(i, stage):
        slab = slabs[i]
        axis = slab.order[stage]
        piece = slab.piece(stage)
        here = coordinate(me, axis)
        for copy in pending[i]:
            copy.wait_recv()
        base = offs[i] + here * piece
        step = min(piece, 32)

        def add(k, _):
            at = k * step
            if stage == 0:
                total = slab.src[rows_at(slab.row0 + base + at, step), :]
            else:
                total = held[i][rows_at(base + at, step), :]
            for d in range(AXES[axis][0] - 1):
                total = total + land[4 * i + stage][d, rows_at(at, step), :]
            if stage == 0:
                held[i][rows_at(at, step), :] = total
            elif stage == 3:
                slab.dst[rows_at(slab.row0 + home[i] + at, step), :] = total
            else:
                held[i][rows_at(base + at, step), :] = total
            return 0

        if stage == 0:
            home[i] = here * piece
        else:
            home[i] = home[i] + here * piece
        lax.fori_loop(0, piece // step, add, 0)
        offs[i] = 0 if stage == 0 else base

    home = [0] * n

    for i in range(n):
        scatter(i, 0)
    for stage in range(4):
        for i in range(n):
            absorb(i, stage)
            if stage < 3:
                scatter(i, stage + 1)
            else:
                spread(i, 3, slabs, home, me, send, pending)
    for stage in (2, 1, 0):
        for i in range(n):
            for copy in pending[i]:
                copy.wait_recv()
            here = coordinate(me, slabs[i].order[stage + 1])
            home[i] = home[i] - here * slabs[i].piece(stage + 1)
            spread(i, stage, slabs, home, me, send, pending)
    for i in range(n):
        for copy in pending[i]:
            copy.wait_recv()
    for copy in started:
        copy.wait_send()


def spread(i, stage, slabs, home, me, send, pending):
    slab = slabs[i]
    axis = slab.order[stage]
    piece = slab.piece(stage)
    view = slab.dst.at[rows_at(slab.row0 + home[i], piece)]
    pending[i] = [send(view, view, peer_of(me, axis, d)) for d in range(1, AXES[axis][0])]


def sum_over_devices(dw_img, dw_txt, small, sub=2):
    plan = sum_plan(dw_img.shape[0], dw_txt.shape[0], sub)
    arrays = [dw_img, dw_txt, small]
    held, land = [], []
    copies = 0
    for a, _, rows, order in plan:
        width = arrays[a].shape[1]
        slab = Slab(None, None, 0, rows, order)
        held.append(pltpu.VMEM((slab.piece(0), width), jnp.float32))
        for stage in range(4):
            others = AXES[order[stage]][0] - 1
            land.append(pltpu.VMEM((others, slab.piece(stage), width), jnp.float32))
            copies += 2 * others
    return pl.pallas_call(
        functools.partial(sum_kernel, plan),
        out_shape=[jax.ShapeDtypeStruct(a.shape, jnp.float32) for a in arrays],
        in_specs=[pl.BlockSpec(memory_space=pltpu.VMEM)] * 3,
        out_specs=[pl.BlockSpec(memory_space=pltpu.VMEM)] * 3,
        scratch_shapes=held + land + [pltpu.SemaphoreType.DMA((copies,)), pltpu.SemaphoreType.DMA((copies,))],
        compiler_params=pltpu.CompilerParams(
            collective_id=1, has_side_effects=True, vmem_limit_bytes=60 * 1024 * 1024),
    )(*arrays)


ID_ROWS = 16


def with_ids(block, ids):
    rows, width = block.shape
    digits = jnp.stack([lax.div(ids, 128), lax.rem(ids, 128)]).astype(jnp.bfloat16)
    digits = jnp.pad(digits, ((0, ID_ROWS - 2), (0, width - rows)))
    return jnp.concatenate([block, digits], axis=0)


def cross_kernel(scal_ref, img_in, txt_in, w_ref, img_out, txt_out, sums_ref,
                 img_all, txt_all, own_txt, emb, grad_ref, rid_img, rid_txt, acc_img, acc_txt, land_img, land_txt,
                 img_send, img_recv, txt_send, txt_recv, swap_send, swap_recv, copy_sem):
    rows = own_txt.shape[1]
    me = lax.axis_index("data")
    core, col_x, col_y, lev = (coordinate(me, a) for a in "cxyz")
    scale = scal_ref[0]
    bias = scal_ref[1]

    load_img = pltpu.make_async_copy(img_in, img_all.at[lev * 4 + col_x * 2 + core], copy_sem.at[0])
    load_txt = pltpu.make_async_copy(txt_in, txt_all.at[lev * 4 + col_y * 2 + core], copy_sem.at[1])
    load_img.start()
    load_txt.start()

    barrier = pltpu.get_barrier_semaphore()
    for axis in "cxy":
        pl.semaphore_signal(barrier, inc=1, device_id=(peer_of(me, axis, 1),), device_id_type=MESH_ID)

    @pl.when(lev > 0)
    def _():
        pl.semaphore_signal(barrier, inc=1, device_id=(me - 8,), device_id_type=MESH_ID)

    @pl.when(lev < 3)
    def _():
        pl.semaphore_signal(barrier, inc=1, device_id=(me + 8,), device_id_type=MESH_ID)

    pl.semaphore_wait(barrier, 3 + jnp.where(lev > 0, 1, 0) + jnp.where(lev < 3, 1, 0))

    class Stream:
        def __init__(self, buf, send_sem, recv_sem, axis):
            self.buf, self.send_sem, self.recv_sem, self.axis = buf, send_sem, recv_sem, axis
            self.side = coordinate(me, axis)
            self.peers = (me + 8, me - 8, peer_of(me, axis, 1), peer_of(me, "c", 1))

        def slot(self, level, near, same_core):
            side = jnp.where(near, self.side, 1 - self.side)
            return level * 4 + side * 2 + jnp.where(same_core, core, 1 - core)

        def copy(self, slot, target):
            return pltpu.make_async_remote_copy(
                src_ref=self.buf.at[slot], dst_ref=self.buf.at[slot],
                send_sem=self.send_sem.at[slot * 4 + target], recv_sem=self.recv_sem.at[slot],
                device_id=(self.peers[target],), device_id_type=MESH_ID)

        def each_target(self, level, near, act):
            slot = self.slot(level, near, True)
            if near:
                @pl.when((level <= lev) & (lev < 3))
                def _():
                    act(self.copy(slot, 0))

                @pl.when((level >= lev) & (lev > 0))
                def _():
                    act(self.copy(slot, 1))

                act(self.copy(slot, 2))
            act(self.copy(slot, 3))

        def arrive(self, level, near, same_core):
            self.copy(self.slot(level, near, same_core), 3).wait_recv()

        def relay(self, dist, near):
            for sign in (-1, 1):
                level = lev + sign * dist
                valid = (level >= 0) & (level <= 3)
                if sign == -1:
                    valid = valid & (dist > 0)

                @pl.when(valid)
                def _():
                    if near:
                        @pl.when(dist > 0)
                        def _():
                            self.arrive(level, True, True)
                    else:
                        self.arrive(level, False, True)
                    self.each_target(level, near, lambda c: c.start())

    txt = Stream(txt_all, txt_send, txt_recv, "y")
    img = Stream(img_all, img_send, img_recv, "x")

    load_txt.wait()
    txt.relay(0, True)
    load_img.wait()
    img.relay(0, True)

    sums_ref[...] = jnp.zeros_like(sums_ref)
    acc_img[...] = jnp.zeros_like(acc_img)
    acc_txt[...] = jnp.zeros_like(acc_txt)

    def id_row(buf, slot):
        digits = buf[slot, pl.ds(rows, ID_ROWS), pl.ds(0, rows)].astype(jnp.float32)
        return digits[0:1] * 128.0 + digits[1:2]

    def id_tile(buf, slot):
        return jnp.transpose(jnp.broadcast_to(id_row(buf, slot), (COL_CHUNK, rows)))

    def embed_block(slot, dst):
        for cc in range(rows // COL_CHUNK):
            sl = pl.ds(cc * COL_CHUNK, COL_CHUNK)
            raw = jnp.dot(txt_all[slot, sl, :], w_ref[...], preferred_element_type=jnp.float32)
            inv = lax.rsqrt(jnp.sum(raw * raw, axis=1, keepdims=True))
            dst[sl, :] = (raw * inv).astype(jnp.bfloat16)

    def block_pass(row_view, rid, acc, col_view, cid, with_loss):
        for half in range(2):
            for rc in range(rows // ROW_CHUNK):
                rsl = pl.ds(rc * ROW_CHUNK, ROW_CHUNK)
                gsl = pl.ds(half * rows + rc * ROW_CHUNK, ROW_CHUNK)
                for cc in range(rows // COL_CHUNK):
                    csl = pl.ds(cc * COL_CHUNK, COL_CHUNK)
                    sim = lax.dot_general(row_view(half)[rsl, :], col_view[csl, :], CONTRACT_COLS,
                                          preferred_element_type=jnp.float32)
                    match = rid[half, rsl, :] == cid[:, cc * COL_CHUNK:(cc + 1) * COL_CHUNK]
                    margin = sim * scale + bias
                    margin = jnp.where(match, -margin, margin)
                    if with_loss:
                        expo = jnp.exp2(-jnp.abs(margin))
                        recip = 1.0 / (1.0 + expo)
                        sig = jnp.where(margin >= 0.0, recip, expo * recip)
                        grad = jnp.where(match, -sig, sig)
                        sums_ref[0] += fold_rows(jnp.maximum(margin, 0.0))
                        sums_ref[1] += log1p_sum(expo)
                        sums_ref[2] += fold_rows(grad * sim)
                        sums_ref[3] += fold_rows(grad)
                    else:
                        sig = 1.0 / (1.0 + jnp.exp2(-margin))
                        grad = jnp.where(match, -sig, sig)
                    grad_ref[gsl, csl] = grad.astype(jnp.bfloat16)
                acc[half, rsl, :] += jnp.dot(grad_ref[gsl, :], col_view[pl.ds(0, rows), :],
                                             preferred_element_type=jnp.float32)

    own_slots = [img.slot(lev, True, True), img.slot(lev, False, True)]
    txt_slots = [txt.slot(lev, True, True), txt.slot(lev, False, True)]

    def level_at(k):
        inner = (lev == 1) | (lev == 2)
        near_low = jnp.where(inner & (k < 2), 1 - k, k)
        return jnp.where(lev >= 2, 3 - near_low, near_low)

    def round_body(k, _):
        level = level_at(k)

        @pl.when(k > 0)
        def _():
            txt.relay(k, True)

        def run_txt(j, _):
            near = j < 2
            same = lax.rem(j, 2) == 0

            @pl.when(j == 0)
            def _():
                @pl.when(k == 0)
                def _():
                    img.relay(0, False)
                    txt.relay(0, False)
                    embed_block(txt_slots[0], own_txt.at[0])
                    embed_block(txt_slots[1], own_txt.at[1])
                    for half in range(2):
                        rid_img[half] = id_tile(img_all, own_slots[half])
                        rid_txt[half] = id_tile(txt_all, txt_slots[half])

            @pl.when(j == 2)
            def _():
                @pl.when(k > 0)
                def _():
                    img.relay(k, True)
                    txt.relay(k, False)

            @pl.when(jnp.logical_not(same))
            def _():
                txt.arrive(level, near, False)

            slot = txt.slot(level, near, same)
            embed_block(slot, emb)
            block_pass(lambda half: img_all.at[own_slots[half]], rid_img, acc_img, emb, id_row(txt_all, slot), True)
            return 0

        lax.fori_loop(0, 4, run_txt, 0)

        def run_img(j, _):
            near = j < 2
            same = lax.rem(j, 2) == 0

            @pl.when((j == 2) & (k > 0))
            def _():
                img.relay(k, False)

            @pl.when(jnp.logical_not(same))
            def _():
                img.arrive(level, near, False)

            slot = img.slot(level, near, same)
            block_pass(lambda half: own_txt.at[half], rid_txt, acc_txt, img_all.at[slot], id_row(img_all, slot), False)
            return 0

        @pl.when(k == 3)
        def _():
            swap(acc_img, land_img, "x", 0).start()

        lax.fori_loop(0, 4, run_img, 0)
        return 0

    def swap(acc, land, axis, k):
        return pltpu.make_async_remote_copy(
            src_ref=acc.at[1], dst_ref=land, send_sem=swap_send.at[k], recv_sem=swap_recv.at[k],
            device_id=(peer_of(me, axis, 1),), device_id_type=MESH_ID)

    lax.fori_loop(0, 4, round_body, 0)

    swap_img = swap(acc_img, land_img, "x", 0)
    swap_txt = swap(acc_txt, land_txt, "y", 1)
    swap_txt.start()

    def settle(level, _):
        for stream in (txt, img):
            for near in (True, False):
                stream.each_target(level, near, lambda c: c.wait_send())
        return 0

    lax.fori_loop(0, 4, settle, 0)
    swap_img.wait()
    img_out[...] = acc_img[0] + land_img[...]
    swap_txt.wait()
    txt_out[...] = acc_txt[0] + land_txt[...]


def cross_pass(scalars, img_block, txt_block, w_txt):
    rows, emb = img_block.shape[0] - ID_ROWS, img_block.shape[1]
    width = txt_block.shape[1]
    full = rows + ID_ROWS
    f32, bf16 = jnp.float32, jnp.bfloat16
    dma = pltpu.SemaphoreType.DMA
    return pl.pallas_call(
        cross_kernel,
        out_shape=[jax.ShapeDtypeStruct((rows, emb), f32), jax.ShapeDtypeStruct((rows, emb), f32),
                   jax.ShapeDtypeStruct((4, 8, COL_CHUNK), f32)],
        in_specs=[pl.BlockSpec(memory_space=pltpu.SMEM), pl.BlockSpec(memory_space=pl.ANY),
                  pl.BlockSpec(memory_space=pl.ANY), pl.BlockSpec(memory_space=pltpu.VMEM)],
        out_specs=[pl.BlockSpec(memory_space=pltpu.VMEM)] * 3,
        scratch_shapes=[
            pltpu.VMEM((16, full, emb), bf16), pltpu.VMEM((16, full, width), bf16),
            pltpu.VMEM((2, rows, emb), bf16), pltpu.VMEM((rows, emb), bf16), pltpu.VMEM((2 * rows, rows), bf16),
            pltpu.VMEM((2, rows, COL_CHUNK), f32), pltpu.VMEM((2, rows, COL_CHUNK), f32),
            pltpu.VMEM((2, rows, emb), f32), pltpu.VMEM((2, rows, emb), f32),
            pltpu.VMEM((rows, emb), f32), pltpu.VMEM((rows, emb), f32),
            dma((64,)), dma((16,)), dma((64,)), dma((16,)), dma((2,)), dma((2,)), dma((2,)),
        ],
        compiler_params=pltpu.CompilerParams(
            collective_id=0, has_side_effects=True, vmem_limit_bytes=62 * 1024 * 1024),
    )(scalars, img_block, txt_block, w_txt)


def solution(mesh):
    n_dev = mesh.shape["data"]

    def local_fn(feat_img, feat_txt, w_img, w_txt, log_temp, logit_bias, pair_ids):
        total_rows = feat_img.shape[0] * n_dev
        temp_scale = jnp.exp(log_temp)
        scalars = jnp.stack([temp_scale * LOG2E, logit_bias * LOG2E])
        unit_img, inv_img, emb_img = embed_rows(feat_img, w_img)
        unit_txt, inv_txt, _ = embed_rows(feat_txt, w_txt)
        acc_img, acc_txt, sums = cross_pass(scalars, with_ids(emb_img, pair_ids), with_ids(feat_txt, pair_ids), w_txt)
        out_scale = temp_scale / total_rows
        dw_img = weight_grad(feat_img, unit_img, inv_img, out_scale * acc_img)
        dw_txt = weight_grad(feat_txt, unit_txt, inv_txt, out_scale * acc_txt)
        sums = jnp.sum(sums, axis=(1, 2))
        small = jnp.stack([LN2 * sums[0] + sums[1], sums[2], sums[3]]) / total_rows
        small = jnp.pad(small[:, None], ((0, 253), (0, 127)))
        dw_img, dw_txt, small = sum_over_devices(dw_img, dw_txt, small)
        return small[0, 0], temp_scale * small[1, 0], small[2, 0], dw_img, dw_txt

    return jax.shard_map(
        local_fn,
        mesh=mesh,
        in_specs=(P("data", None), P("data", None), P(None, None), P(None, None), P(), P(), P("data")),
        out_specs=(P(), P(), P(), P(None, None), P(None, None)),
        check_vma=False,
    )
```

time: 1870 us -> 422 us (0.23)
  waiting for transfers between devices: 1200 us -> 0 us
  matrix products: 462 us -> 15.7 us
  Pallas kernels: 0 us -> 376 us
  loops' own time: 61.3 us -> 0 us
  local copies, waits for them, and re-layouts: 64.1 us -> 14.9 us
  blocking collectives: 38.1 us -> 0 us
    ppermute x94 -> x0, waiting for transfers between devices: 1050 us -> none  [the longest x93 1020 us: visit_block(): lax.ppermute((txt_blk, ids_blk, acc_txt + part_txt), 'data', next_perm)]
    dot_general x96 -> x0, matrix products: 448 us -> none  [the longest x32 161 us: tile_terms(): part_img = jnp.dot(grad_bf, emb_txt, preferred_element_type=jnp.float32)]
    pallas_call x0 -> x2, Pallas kernels: none -> 376 us  [the longest x1 245 us: cross_pass(): pl.pallas_call(cross_kernel, out_shape=[jax.ShapeDtypeStruct((rows, emb),...]
    psum x1 -> x0, waiting for transfers between devices: 158 us -> none  [local_fn(): lax.psum((loss_sum + loss_part, temp_sum + temp_part, bias_sum + bias_par...]
    another operation x1 -> x0, loops' own time: 61.3 us -> none  [local_fn(): loop_state = lax.fori_loop(0, n_dev - 1, visit_block, loop_state)]
    while x186 -> x0, local copies, waits for them, and re-layouts: 49.5 us -> none
    psum x1 -> x0, blocking collectives: 38.1 us -> none  [local_fn(): lax.psum((loss_sum + loss_part, temp_sum + temp_part, bias_sum + bias_par...]
  transfers between devices with their start and end apart: 95 -> 0, of which waited for: 33 -> 0; matrix products, arithmetic and copies ran while one was open for 9% -> 0% of each run, Pallas kernels for 0% -> 0%
where the time goes in v1:
time: 422 us
  Pallas kernels  376 us (89%)
  matrix products  15.7 us (4%)
  local copies, waits for them, and re-layouts  14.9 us (4%)
  other arithmetic  9.67 us (2%)
  between operations  5.15 us (1%)
    pallas_call x1, Pallas kernels, cross_pass(): pl.pallas_call(cross_kernel, out_shape=[jax.ShapeDtypeStruct((rows, emb),...  245 us
    pallas_call x1, Pallas kernels, sum_over_devices(): pl.pallas_call(functools.partial(sum_kernel, plan), out_shape=[jax.ShapeD...  132 us
    unnamed x20, local copies, waits for them, and re-layouts  12.2 us

profile of v1, /device:TPU:0, one launch (start us, length us, event | category | flops | bytes accessed | tf_op | source)
XLA Modules:
  0.0 421.6 jit_solution(1696597347670689739)
XLA Ops:
  2.0 0.6 pad_maximum_fusion.1.scal_ref
  2.6 0.7 fusion.10
  3.3 1.9 fusion.9.txt_in
  5.2 5.2 %multiply_reduce_fusion.3 = (f32[512]{0:T(512)S(1)}, f32[512,1024]{1,0:T(8,128)S(1)}) fusion(bf16[512,2048]{1,0:T(8,128)(2,1)} %param.7, bf16[2048,1024]{1,0:T(8,128)(2,1)} %param.9), kind=kOutput, calls=%fused_computation.8 | convolution fusion | flops 2148531712 | bytes 8390656 | tf_op jit(solution)/shard_map/dot_general | solution.py:19
  10.4 0.2 multiply_convert_fusion.2
  10.6 1.1 fusion.1.img_in
  11.7 0.4 copy-done.1
  12.1 0.9 copy-done.6
  13.0 2.0 multiply_reduce_fusion.1
  15.0 244.5 %shard_map.115 = (f32[512,1024]{1,0:T(8,128)}, f32[512,1024]{1,0:T(8,128)}, f32[4,8,256]{2,1,0:T(8,128)}) custom-call(f32[2]{0:T(128)} %pad_maximum_fusion.1.scal_ref, bf16[528,1024]{1,0:T(8,128)(2,1)} %fusion.1.img_in, bf16[528,512]{1,0:T(8,128)(2,1)} %fusion.9.txt_in, bf16[512,1024]{1,0:T(8,128)(2,1)} %w_ref.1), custom_call_target="tpu_custom_call" | custom-call | tf_op jit(solution)/shard_map/pallas_call | solution.py:469
  259.5 0.9 reduce_sum.49
  260.5 0.6 fusion.13
  262.4 0.1 pad_maximum_fusion.2
  262.5 0.1 copy.17
  262.6 4.3 %multiply_reduce_fusion = (f32[512]{0:T(512)S(1)}, f32[512]{0:T(512)S(1)}) fusion(f32[512,1024]{1,0:T(8,128)} %get-tuple-element.27, f32[512,1024]{1,0:T(8,128)} %get-tuple-element.12, f32[512]{0:T(512)S(1)} %rsqrt.17, f32[]{:T(128)S(6)} %div.22, f32[512,1024]{1,0:T(8,128)} %get-tuple-element.11, f32[512,1024]{1,0:T(8,128)} %copy-done.1, f32[512]{0:T(512)S(1)} %rsqrt.16), kind=kLoop, calls=%fused_computation.4 | loop fusion | flops 4193280 | bytes 8396804 | tf_op jit(solution)/shard_map/reduce_sum | solution.py:26
  266.9 0.4 copy-done.3
  267.2 2.4 convolution_bitcast_fusion.1.refs_1_
  269.6 0.7 pad.14.refs_2_
  270.3 0.6 copy-done.8
  270.9 6.0 %convolution_bitcast_fusion.refs_0_ = f32[2048,1024]{1,0:T(8,128)} fusion(bf16[512,2048]{1,0:T(8,128)(2,1)S(1)} %copy-done.8, f32[512,1024]{1,0:T(8,128)S(1)} %copy-done.4, f32[512,1024]{1,0:T(8,128)S(1)} %copy-done.2, f32[512]{0:T(512)S(1)} %get-tuple-element.29, f32[]{:T(128)S(6)} %div.22, f32[512]{0:T(512)S(1)} %rsqrt.16), kind=kOutput, calls=%fused_computation | convolution fusion | flops 2150629376 | bytes 14684164 | tf_op jit(solution)/shard_map/dot_general | solution.py:27
  276.9 131.7 %shard_map.116 = (f32[2048,1024]{1,0:T(8,128)}, f32[512,1024]{1,0:T(8,128)}, f32[256,128]{1,0:T(8,128)}) custom-call(f32[2048,1024]{1,0:T(8,128)} %convolution_bitcast_fusion.refs_0_, f32[512,1024]{1,0:T(8,128)} %convolution_bitcast_fusion.1.refs_1_, f32[256,128]{1,0:T(8,128)} %pad.14.refs_2_), custom_call_target="tpu_custom_call" | custom-call | tf_op jit(solution)/shard_map/pallas_call | solution.py:214
  408.6 1.3 fusion.12
  410.6 8.6 %copy.24 = f32[2048,1024]{1,0:T(8,128)} copy(f32[2048,1024]{1,0:T(8,128)} %get-tuple-element.38) | data formatting | bytes 16777216
  419.2 1.3 copy.25
  (21 shorter events, 0.1 us)
Async XLA Ops:
  10.4 1.7 copy-start.1
  10.4 1.7 copy-start.5
  10.4 2.5 copy-start.6
  262.6 4.3 %copy-start = (f32[512,1024]{1,0:T(8,128)S(1)}, f32[512,1024]{1,0:T(8,128)}, u32[]{:S(2)}) copy-start(f32[512,1024]{1,0:T(8,128)} %get-tuple-element.27) | copy-start | bytes 6291460
  262.6 4.7 %copy-start.3 = (f32[512,1024]{1,0:T(8,128)S(1)}, f32[512,1024]{1,0:T(8,128)}, u32[]{:S(2)}) copy-start(f32[512,1024]{1,0:T(8,128)} %get-tuple-element.12) | copy-start | bytes 6291460
  267.2 3.0 copy-start.2
  267.2 3.0 copy-start.4
  267.2 3.7 copy-start.8
  410.6 8.6 %copy-start.7 = (f32[512,1024]{1,0:T(8,128)S(1)}, f32[512,1024]{1,0:T(8,128)}, u32[]{:S(2)}) copy-start(f32[512,1024]{1,0:T(8,128)} %get-tuple-element.39) | copy-start | bytes 6291460

commit v2 on v1

--- a/solution.py
+++ b/solution.py
@@ -11,7 +11,6 @@
 CONTRACT_COLS = (((1,), (1,)), ((), ()))
 LOG2E = 1.4426950408889634
 LN2 = 0.6931471805599453
-ROW_CHUNK = 256
 COL_CHUNK = 256
 
 
@@ -223,6 +222,17 @@
 
 
 ID_ROWS = 16
+PIECES = {"T": 1, "I": 2}
+SCHEDULE = (
+    "RT00", "RI00", "RT10", "BT00", "RI01", "BI00", "BI01", "RI10",
+    "I0b1", "I0n1", "RT20", "T2n1", "T1n0", "T0b1", "RI11", "BT10",
+    "T0n0", "T1n1", "T1b1", "RI20", "BI10", "BT20", "T0n1", "T2b1",
+    "RT30", "T2b0", "BI11", "RI21", "T1b0", "T3n1", "RI30", "I2n1",
+    "BT30", "BI20", "I1b1", "T3b1", "BI21", "RI31", "SI", "I3n1",
+    "I1n1", "BI30", "I2b1", "BI31", "I3b1", "ST", "I2b0", "T0b0",
+    "T2n0", "I0b0", "I2n0", "I1n0", "T3n0", "I1b0", "I3b0", "I0n0",
+    "I3n0", "T3b0",
+)
 
 
 def with_ids(block, ids):
@@ -261,8 +271,9 @@
     pl.semaphore_wait(barrier, 3 + jnp.where(lev > 0, 1, 0) + jnp.where(lev < 3, 1, 0))
 
     class Stream:
-        def __init__(self, buf, send_sem, recv_sem, axis):
-            self.buf, self.send_sem, self.recv_sem, self.axis = buf, send_sem, recv_sem, axis
+        def __init__(self, kind, buf, send_sem, recv_sem, axis):
+            self.pieces = PIECES[kind]
+            self.buf, self.send_sem, self.recv_sem = buf, send_sem, recv_sem
             self.side = coordinate(me, axis)
             self.peers = (me + 8, me - 8, peer_of(me, axis, 1), peer_of(me, "c", 1))
 
@@ -270,53 +281,64 @@
             side = jnp.where(near, self.side, 1 - self.side)
             return level * 4 + side * 2 + jnp.where(same_core, core, 1 - core)
 
-        def copy(self, slot, target):
+        def copy(self, slot, target, piece):
+            share = rows // self.pieces
+            size = share + (ID_ROWS if piece == self.pieces - 1 else 0)
+            part = self.buf.at[slot, pl.ds(piece * share, size)]
             return pltpu.make_async_remote_copy(
-                src_ref=self.buf.at[slot], dst_ref=self.buf.at[slot],
-                send_sem=self.send_sem.at[slot * 4 + target], recv_sem=self.recv_sem.at[slot],
+                src_ref=part, dst_ref=part,
+                send_sem=self.send_sem.at[(slot * 4 + target) * self.pieces + piece],
+                recv_sem=self.recv_sem.at[slot * self.pieces + piece],
                 device_id=(self.peers[target],), device_id_type=MESH_ID)
 
-        def each_target(self, level, near, act):
+        def each_target(self, level, near, piece, act):
             slot = self.slot(level, near, True)
             if near:
                 @pl.when((level <= lev) & (lev < 3))
                 def _():
-                    act(self.copy(slot, 0))
+                    act(self.copy(slot, 0, piece))
 
                 @pl.when((level >= lev) & (lev > 0))
                 def _():
-                    act(self.copy(slot, 1))
-
-                act(self.copy(slot, 2))
-            act(self.copy(slot, 3))
-
-        def arrive(self, level, near, same_core):
-            self.copy(self.slot(level, near, same_core), 3).wait_recv()
-
-        def relay(self, dist, near):
-            for sign in (-1, 1):
+                    act(self.copy(slot, 1, piece))
+
+                act(self.copy(slot, 2, piece))
+            act(self.copy(slot, 3, piece))
+
+        def arrive(self, level, near, same_core, piece):
+            self.copy(self.slot(level, near, same_core), 3, piece).wait_recv()
+
+        def relay(self, dist, near, piece):
+            for sign in (-1, 1) if dist else (1,):
                 level = lev + sign * dist
-                valid = (level >= 0) & (level <= 3)
-                if sign == -1:
-                    valid = valid & (dist > 0)
-
-                @pl.when(valid)
+
+                @pl.when((level >= 0) & (level <= 3))
                 def _():
-                    if near:
-                        @pl.when(dist > 0)
-                        def _():
-                            self.arrive(level, True, True)
-                    else:
-                        self.arrive(level, False, True)
-                    self.each_target(level, near, lambda c: c.start())
-
-    txt = Stream(txt_all, txt_send, txt_recv, "y")
-    img = Stream(img_all, img_send, img_recv, "x")
+                    if dist > 0 or not near:
+                        self.arrive(level, near, True, piece)
+                    self.each_target(level, near, piece, lambda c: c.start())
+
+    txt = Stream("T", txt_all, txt_send, txt_recv, "y")
+    img = Stream("I", img_all, img_send, img_recv, "x")
+    streams = {"T": txt, "I": img}
+
+    def swap(acc, land, axis, k):
+        return pltpu.make_async_remote_copy(
+            src_ref=acc.at[1], dst_ref=land, send_sem=swap_send.at[k], recv_sem=swap_recv.at[k],
+            device_id=(peer_of(me, axis, 1),), device_id_type=MESH_ID)
+
+    swaps = {"I": swap(acc_img, land_img, "x", 0), "T": swap(acc_txt, land_txt, "y", 1)}
+
+    def level_at(k):
+        inner = (lev == 1) | (lev == 2)
+        near_low = jnp.where(inner & (k < 2), 1 - k, k)
+        return jnp.where(lev >= 2, 3 - near_low, near_low)
 
     load_txt.wait()
-    txt.relay(0, True)
+    txt.relay(0, True, 0)
     load_img.wait()
-    img.relay(0, True)
+    for piece in range(img.pieces):
+        img.relay(0, True, piece)
 
     sums_ref[...] = jnp.zeros_like(sums_ref)
     acc_img[...] = jnp.zeros_like(acc_img)
@@ -336,127 +358,108 @@
             inv = lax.rsqrt(jnp.sum(raw * raw, axis=1, keepdims=True))
             dst[sl, :] = (raw * inv).astype(jnp.bfloat16)
 
-    def block_pass(row_view, rid, acc, col_view, cid, with_loss):
+    def block_pass(row_view, rid, acc, half, col_views, cids, with_loss):
+        for part in range(2):
+            for cc in range(rows // COL_CHUNK):
+                csl = pl.ds(cc * COL_CHUNK, COL_CHUNK)
+                sim = lax.dot_general(row_view[pl.ds(0, rows), :], col_views[part][csl, :], CONTRACT_COLS,
+                                      preferred_element_type=jnp.float32)
+                match = rid[half] == cids[part][:, cc * COL_CHUNK:(cc + 1) * COL_CHUNK]
+                margin = sim * scale + bias
+                margin = jnp.where(match, -margin, margin)
+                if with_loss:
+                    expo = jnp.exp2(-jnp.abs(margin))
+                    recip = 1.0 / (1.0 + expo)
+                    sig = jnp.where(margin >= 0.0, recip, expo * recip)
+                    grad = jnp.where(match, -sig, sig)
+                    sums_ref[0] += fold_rows(jnp.maximum(margin, 0.0))
+                    sums_ref[1] += log1p_sum(expo)
+                    sums_ref[2] += fold_rows(grad * sim)
+                    sums_ref[3] += fold_rows(grad)
+                else:
+                    sig = 1.0 / (1.0 + jnp.exp2(-margin))
+                    grad = jnp.where(match, -sig, sig)
+                grad_ref[:, pl.ds(part * rows + cc * COL_CHUNK, COL_CHUNK)] = grad.astype(jnp.bfloat16)
+        total = jnp.dot(grad_ref[:, pl.ds(0, rows)], col_views[0][pl.ds(0, rows), :],
+                        preferred_element_type=jnp.float32)
+        total += jnp.dot(grad_ref[:, pl.ds(rows, rows)], col_views[1][pl.ds(0, rows), :],
+                         preferred_element_type=jnp.float32)
+        acc[half] += total
+
+    def prepare():
         for half in range(2):
-            for rc in range(rows // ROW_CHUNK):
-                rsl = pl.ds(rc * ROW_CHUNK, ROW_CHUNK)
-                gsl = pl.ds(half * rows + rc * ROW_CHUNK, ROW_CHUNK)
-                for cc in range(rows // COL_CHUNK):
-                    csl = pl.ds(cc * COL_CHUNK, COL_CHUNK)
-                    sim = lax.dot_general(row_view(half)[rsl, :], col_view[csl, :], CONTRACT_COLS,
-                                          preferred_element_type=jnp.float32)
-                    match = rid[half, rsl, :] == cid[:, cc * COL_CHUNK:(cc + 1) * COL_CHUNK]
-                    margin = sim * scale + bias
-                    margin = jnp.where(match, -margin, margin)
-                    if with_loss:
-                        expo = jnp.exp2(-jnp.abs(margin))
-                        recip = 1.0 / (1.0 + expo)
-                        sig = jnp.where(margin >= 0.0, recip, expo * recip)
-                        grad = jnp.where(match, -sig, sig)
-                        sums_ref[0] += fold_rows(jnp.maximum(margin, 0.0))
-                        sums_ref[1] += log1p_sum(expo)
-                        sums_ref[2] += fold_rows(grad * sim)
-                        sums_ref[3] += fold_rows(grad)
-                    else:
-                        sig = 1.0 / (1.0 + jnp.exp2(-margin))
-                        grad = jnp.where(match, -sig, sig)
-                    grad_ref[gsl, csl] = grad.astype(jnp.bfloat16)
-                acc[half, rsl, :] += jnp.dot(grad_ref[gsl, :], col_view[pl.ds(0, rows), :],
-                                             preferred_element_type=jnp.float32)
-
-    own_slots = [img.slot(lev, True, True), img.slot(lev, False, True)]
-    txt_slots = [txt.slot(lev, True, True), txt.slot(lev, False, True)]
-
-    def level_at(k):
-        inner = (lev == 1) | (lev == 2)
-        near_low = jnp.where(inner & (k < 2), 1 - k, k)
-        return jnp.where(lev >= 2, 3 - near_low, near_low)
-
-    def round_body(k, _):
-        level = level_at(k)
-
-        @pl.when(k > 0)
+            slot = txt.slot(lev, half == 0, True)
+            embed_block(slot, own_txt.at[half])
+            rid_img[half] = id_tile(img_all, img.slot(lev, half == 0, True))
+            rid_txt[half] = id_tile(txt_all, slot)
+
+    before, codes, seen = [[]], [], set()
+    for word in SCHEDULE:
+        if word[0] in "RB":
+            if word[0] == "B" or word[2] != "0":
+                stream, dist, piece = streams[word[1]], int(word[2]), int(word[3])
+                before[-1].append(functools.partial(stream.relay, dist, word[0] == "R", piece))
+        elif word[0] == "S":
+            before[-1].append(swaps[word[1]].start)
+        else:
+            kind, k, near, half = word[0], int(word[1]), word[2] == "n", int(word[3])
+            if not codes:
+                before[-1].append(prepare)
+            if word[:3] not in seen:
+                seen.add(word[:3])
+                for piece in range(PIECES[kind]):
+                    before[-1].append(functools.partial(
+                        lambda st, k, near, piece: st.arrive(level_at(k), near, False, piece),
+                        streams[kind], k, near, piece))
+            codes.append((0 if kind == "T" else 16) + k * 4 + (0 if near else 2) + half)
+            before.append([])
+
+    def step(i, _):
+        for at, acts in enumerate(before[:-1]):
+            if acts:
+                @pl.when(i == at)
+                def _():
+                    for act in acts:
+                        act()
+
+        code = jnp.int32(codes[0])
+        for at in range(1, len(codes)):
+            code = jnp.where(i == at, codes[at], code)
+        half = lax.rem(code, 2)
+        near = lax.rem(lax.div(code, 2), 2) == 0
+        level = level_at(lax.rem(lax.div(code, 4), 4))
+
+        @pl.when(code < 16)
         def _():
-            txt.relay(k, True)
-
-        def run_txt(j, _):
-            near = j < 2
-            same = lax.rem(j, 2) == 0
-
-            @pl.when(j == 0)
-            def _():
-                @pl.when(k == 0)
-                def _():
-                    img.relay(0, False)
-                    txt.relay(0, False)
-                    embed_block(txt_slots[0], own_txt.at[0])
-                    embed_block(txt_slots[1], own_txt.at[1])
-                    for half in range(2):
-                        rid_img[half] = id_tile(img_all, own_slots[half])
-                        rid_txt[half] = id_tile(txt_all, txt_slots[half])
-
-            @pl.when(j == 2)
-            def _():
-                @pl.when(k > 0)
-                def _():
-                    img.relay(k, True)
-                    txt.relay(k, False)
-
-            @pl.when(jnp.logical_not(same))
-            def _():
-                txt.arrive(level, near, False)
-
-            slot = txt.slot(level, near, same)
-            embed_block(slot, emb)
-            block_pass(lambda half: img_all.at[own_slots[half]], rid_img, acc_img, emb, id_row(txt_all, slot), True)
-            return 0
-
-        lax.fori_loop(0, 4, run_txt, 0)
-
-        def run_img(j, _):
-            near = j < 2
-            same = lax.rem(j, 2) == 0
-
-            @pl.when((j == 2) & (k > 0))
-            def _():
-                img.relay(k, False)
-
-            @pl.when(jnp.logical_not(same))
-            def _():
-                img.arrive(level, near, False)
-
-            slot = img.slot(level, near, same)
-            block_pass(lambda half: own_txt.at[half], rid_txt, acc_txt, img_all.at[slot], id_row(img_all, slot), False)
-            return 0
-
-        @pl.when(k == 3)
+            slots = [txt.slot(level, near, same) for same in (True, False)]
+            for part in range(2):
+                embed_block(slots[part], emb.at[part])
+            block_pass(img_all.at[img.slot(lev, half == 0, True)], rid_img, acc_img, half, [emb.at[0], emb.at[1]],
+                       [id_row(txt_all, slot) for slot in slots], True)
+
+        @pl.when(code >= 16)
         def _():
-            swap(acc_img, land_img, "x", 0).start()
-
-        lax.fori_loop(0, 4, run_img, 0)
+            slots = [img.slot(level, near, same) for same in (True, False)]
+            block_pass(own_txt.at[half], rid_txt, acc_txt, half, [img_all.at[slot] for slot in slots],
+                       [id_row(img_all, slot) for slot in slots], False)
+
         return 0
 
-    def swap(acc, land, axis, k):
-        return pltpu.make_async_remote_copy(
-            src_ref=acc.at[1], dst_ref=land, send_sem=swap_send.at[k], recv_sem=swap_recv.at[k],
-            device_id=(peer_of(me, axis, 1),), device_id_type=MESH_ID)
-
-    lax.fori_loop(0, 4, round_body, 0)
-
-    swap_img = swap(acc_img, land_img, "x", 0)
-    swap_txt = swap(acc_txt, land_txt, "y", 1)
-    swap_txt.start()
+    lax.fori_loop(0, len(codes), step, 0)
+    for act in before[-1]:
+        act()
 
     def settle(level, _):
         for stream in (txt, img):
             for near in (True, False):
-                stream.each_target(level, near, lambda c: c.wait_send())
+                for piece in range(stream.pieces):
+                    stream.each_target(level, near, piece, lambda c: c.wait_send())
         return 0
 
     lax.fori_loop(0, 4, settle, 0)
-    swap_img.wait()
+    swaps["I"].wait()
     img_out[...] = acc_img[0] + land_img[...]
-    swap_txt.wait()
+    swaps["T"].wait()
     txt_out[...] = acc_txt[0] + land_txt[...]
 
 
@@ -475,11 +478,11 @@
         out_specs=[pl.BlockSpec(memory_space=pltpu.VMEM)] * 3,
         scratch_shapes=[
             pltpu.VMEM((16, full, emb), bf16), pltpu.VMEM((16, full, width), bf16),
-            pltpu.VMEM((2, rows, emb), bf16), pltpu.VMEM((rows, emb), bf16), pltpu.VMEM((2 * rows, rows), bf16),
+            pltpu.VMEM((2, rows, emb), bf16), pltpu.VMEM((2, rows, emb), bf16), pltpu.VMEM((rows, 2 * rows), bf16),
             pltpu.VMEM((2, rows, COL_CHUNK), f32), pltpu.VMEM((2, rows, COL_CHUNK), f32),
             pltpu.VMEM((2, rows, emb), f32), pltpu.VMEM((2, rows, emb), f32),
             pltpu.VMEM((rows, emb), f32), pltpu.VMEM((rows, emb), f32),
-            dma((64,)), dma((16,)), dma((64,)), dma((16,)), dma((2,)), dma((2,)), dma((2,)),
+            dma((64 * PIECES["I"],)), dma((16 * PIECES["I"],)), dma((64 * PIECES["T"],)), dma((16 * PIECES["T"],)), dma((2,)), dma((2,)), dma((2,)),
         ],
         compiler_params=pltpu.CompilerParams(
             collective_id=0, has_side_effects=True, vmem_limit_bytes=62 * 1024 * 1024),

time: 422 us -> 365 us (0.86)
  Pallas kernels: 376 us -> 319 us
    pallas_call x1, Pallas kernels: 245 us -> 193 us  [cross_pass(): pl.pallas_call(cross_kernel, out_shape=[jax.ShapeDtypeStruct((rows, emb),...]
    pallas_call x1, Pallas kernels: 132 us -> 126 us  [sum_over_devices(): pl.pallas_call(functools.partial(sum_kernel, plan), out_shape=[jax.ShapeD...]
where the time goes in v2:
time: 365 us; the launch traced here: 364 us
  Pallas kernels  319 us (87%)
  matrix products  15.7 us (4%)
  local copies, waits for them, and re-layouts  14.9 us (4%)
  other arithmetic  9.67 us (3%)
  between operations  5.15 us (1%)
    pallas_call x1, Pallas kernels, cross_pass(): pl.pallas_call(cross_kernel, out_shape=[jax.ShapeDtypeStruct((rows, emb),...  193 us
    pallas_call x1, Pallas kernels, sum_over_devices(): pl.pallas_call(functools.partial(sum_kernel, plan), out_shape=[jax.ShapeD...  126 us
    unnamed x20, local copies, waits for them, and re-layouts  12.2 us
    dot_general x2, matrix products, weight_grad(): lax.dot_general(feat_rows, raw_grad.astype(jnp.bfloat16), CONTRACT_ROWS,...  8.4 us

profile of v2, /device:TPU:0, one launch (start us, length us, event | category | flops | bytes accessed | tf_op | source)
XLA Modules:
  0.0 364.4 jit_solution(14576370450459795281)
XLA Ops:
  2.0 0.6 pad_maximum_fusion.1.scal_ref
  2.6 0.7 fusion.10
  3.3 1.9 fusion.9.txt_in
  5.2 5.2 %multiply_reduce_fusion.3 = (f32[512]{0:T(512)S(1)}, f32[512,1024]{1,0:T(8,128)S(1)}) fusion(bf16[512,2048]{1,0:T(8,128)(2,1)} %param.7, bf16[2048,1024]{1,0:T(8,128)(2,1)} %param.9), kind=kOutput, calls=%fused_computation.8 | convolution fusion | flops 2148531712 | bytes 8390656 | tf_op jit(solution)/shard_map/dot_general | solution.py:18
  10.4 0.2 multiply_convert_fusion.2
  10.6 1.1 fusion.1.img_in
  11.7 0.4 copy-done.1
  12.1 0.9 copy-done.6
  13.0 2.0 multiply_reduce_fusion.1
  15.0 193.3 %shard_map.115 = (f32[512,1024]{1,0:T(8,128)}, f32[512,1024]{1,0:T(8,128)}, f32[4,8,256]{2,1,0:T(8,128)}) custom-call(f32[2]{0:T(128)} %pad_maximum_fusion.1.scal_ref, bf16[528,1024]{1,0:T(8,128)(2,1)} %fusion.1.img_in, bf16[528,512]{1,0:T(8,128)(2,1)} %fusion.9.txt_in, bf16[512,1024]{1,0:T(8,128)(2,1)} %w_ref.1), custom_call_target="tpu_custom_call" | custom-call | tf_op jit(solution)/shard_map/pallas_call | solution.py:472
  208.3 0.9 reduce_sum.49
  209.2 0.1 slice_bitcast_fusion
  209.3 0.6 fusion.13
  211.2 0.1 copy.17
  211.3 4.3 %multiply_reduce_fusion = (f32[512]{0:T(512)S(1)}, f32[512]{0:T(512)S(1)}) fusion(f32[512,1024]{1,0:T(8,128)} %get-tuple-element.27, f32[512,1024]{1,0:T(8,128)} %get-tuple-element.12, f32[512]{0:T(512)S(1)} %rsqrt.17, f32[]{:T(128)S(6)} %div.22, f32[512,1024]{1,0:T(8,128)} %get-tuple-element.11, f32[512,1024]{1,0:T(8,128)} %copy-done.1, f32[512]{0:T(512)S(1)} %rsqrt.16), kind=kLoop, calls=%fused_computation.4 | loop fusion | flops 4193280 | bytes 8396804 | tf_op jit(solution)/shard_map/reduce_sum | solution.py:25
  215.6 0.4 copy-done.3
  216.0 2.4 convolution_bitcast_fusion.1.refs_1_
  218.4 0.7 pad.14.refs_2_
  219.1 0.6 copy-done.8
  219.7 6.0 %convolution_bitcast_fusion.refs_0_ = f32[2048,1024]{1,0:T(8,128)} fusion(bf16[512,2048]{1,0:T(8,128)(2,1)S(1)} %copy-done.8, f32[512,1024]{1,0:T(8,128)S(1)} %copy-done.4, f32[512,1024]{1,0:T(8,128)S(1)} %copy-done.2, f32[512]{0:T(512)S(1)} %get-tuple-element.29, f32[]{:T(128)S(6)} %div.22, f32[512]{0:T(512)S(1)} %rsqrt.16), kind=kOutput, calls=%fused_computation | convolution fusion | flops 2150629376 | bytes 14684164 | tf_op jit(solution)/shard_map/dot_general | solution.py:26
  225.7 125.6 %shard_map.116 = (f32[2048,1024]{1,0:T(8,128)}, f32[512,1024]{1,0:T(8,128)}, f32[256,128]{1,0:T(8,128)}) custom-call(f32[2048,1024]{1,0:T(8,128)} %convolution_bitcast_fusion.refs_0_, f32[512,1024]{1,0:T(8,128)} %convolution_bitcast_fusion.1.refs_1_, f32[256,128]{1,0:T(8,128)} %pad.14.refs_2_), custom_call_target="tpu_custom_call" | custom-call | tf_op jit(solution)/shard_map/pallas_call | solution.py:213
  351.4 1.3 fusion.12
  353.3 8.6 %copy.24 = f32[2048,1024]{1,0:T(8,128)} copy(f32[2048,1024]{1,0:T(8,128)} %get-tuple-element.38) | data formatting | bytes 16777216
  361.9 1.3 copy.25
  (21 shorter events, 0.1 us)
Async XLA Ops:
  10.4 1.7 copy-start.1
  10.4 1.7 copy-start.5
  10.4 2.5 copy-start.6
  211.3 4.3 %copy-start = (f32[512,1024]{1,0:T(8,128)S(1)}, f32[512,1024]{1,0:T(8,128)}, u32[]{:S(2)}) copy-start(f32[512,1024]{1,0:T(8,128)} %get-tuple-element.27) | copy-start | bytes 6291460
  211.3 4.7 %copy-start.3 = (f32[512,1024]{1,0:T(8,128)S(1)}, f32[512,1024]{1,0:T(8,128)}, u32[]{:S(2)}) copy-start(f32[512,1024]{1,0:T(8,128)} %get-tuple-element.12) | copy-start | bytes 6291460
  216.0 3.0 copy-start.2
  216.0 3.0 copy-start.4
  216.0 3.7 %copy-start.8 = (bf16[512,2048]{1,0:T(8,128)(2,1)S(1)}, bf16[512,2048]{1,0:T(8,128)(2,1)}, u32[]{:S(2)}) copy-start(bf16[512,2048]{1,0:T(8,128)(2,1)} %param.7) | copy-start | bytes 6291460
  353.3 8.6 %copy-start.7 = (f32[512,1024]{1,0:T(8,128)S(1)}, f32[512,1024]{1,0:T(8,128)}, u32[]{:S(2)}) copy-start(f32[512,1024]{1,0:T(8,128)} %get-tuple-element.39) | copy-start | bytes 6291460

commit v3 on v2

--- a/solution.py
+++ b/solution.py
@@ -42,8 +42,18 @@
     return terms[0]
 
 
-AXES = {"c": (2, 1), "x": (2, 2), "y": (2, 4), "z": (4, 8)}
+AXES = {"c": (2, 1), "x": (2, 2), "y": (2, 4), "u": (2, 8), "v": (2, 16), "z": (4, 8)}
 MESH_ID = pl.DeviceIdType.MESH
+UNIT = 256
+SUM_ORDERS = ("cyuvx", "cxyuv", "cuxyv", "cxyuv", "cxyvu", "cxyuv", "cyxuv", "cuyxv", "cyuxv", "cxyuv")
+SUM_STEPS = (
+    0, 10, 50, 70, 80, 30, 11, 1, 20, 51, 12, 90, 100, 81, 31, 71, 21, 52, 13, 32,
+    82, 60, 2, 40, 33, 14, 34, 83, 41, 72, 15, 61, 53, 22, 35, 84, 42, 91, 101, 16,
+    23, 36, 62, 3, 85, 54, 73, 92, 102, 24, 17, 43, 4, 63, 55, 93, 103, 44, 74, 86,
+    64, 25, 37, 56, 45, 94, 104, 75, 87, 5, 65, 26, 46, 38, 57, 76, 95, 105, 6, 66,
+    27, 96, 106, 47, 7, 67, 97, 107, 77, 88, 28, 18, 58, 48, 49, 29, 8, 89, 59, 78,
+    98, 108, 39, 9, 68, 19, 99, 109, 69, 79,
+)
 
 
 def coordinate(me, axis):
@@ -51,7 +61,7 @@
     return lax.rem(lax.div(me, stride), size)
 
 
-def peer_of(me, axis, dist):
+def peer_of(me, axis, dist=1):
     size, stride = AXES[axis]
     here = coordinate(me, axis)
     return me + (lax.rem(here + dist, size) - here) * stride
@@ -61,157 +71,100 @@
     return pl.ds(pl.multiple_of(start, 8), size)
 
 
-class Slab:
-    def __init__(self, src, dst, row0, rows, order):
-        self.src, self.dst, self.row0, self.rows, self.order = src, dst, row0, rows, order
-
-    def piece(self, stage):
-        rows = self.rows
-        for axis in self.order[:stage + 1]:
-            rows //= AXES[axis][0]
-        return rows
-
-
-def sum_plan(wi_rows, wt_rows, sub):
-    plan = []
-    for k in range(sub):
-        half = wi_rows // 2 // sub
-        part = wt_rows // sub
-        plan.append((0, k * half, half, "cxyz"))
-        plan.append((0, wi_rows // 2 + k * half, half, "cyxz"))
-        plan.append((1, k * part, part, "czxy"))
-    plan.append((2, 0, 256, "cxyz"))
-    return plan
-
-
-def sum_kernel(plan, *refs):
+def sum_kernel(orders, steps, *refs):
     ins, outs = refs[:3], refs[3:6]
-    n = len(plan)
+    n = len(orders)
     held = refs[6:6 + n]
-    land = refs[6 + n:6 + 5 * n]
-    send_sem, recv_sem = refs[6 + 5 * n:]
+    land = refs[6 + n:6 + 6 * n]
+    send_sem, recv_sem = refs[6 + 6 * n:]
     me = lax.axis_index("data")
-    slabs = [Slab(ins[a], outs[a], row0, rows, order) for a, row0, rows, order in plan]
+    bits = {axis: coordinate(me, axis) for axis in "cxyuv"}
+    peers = {axis: peer_of(me, axis) for axis in "cxyuv"}
+    img_units = ins[0].shape[0] // UNIT
+    txt_units = ins[1].shape[0] // UNIT
+    place = [(0, u * UNIT) for u in range(img_units)] + [(1, u * UNIT) for u in range(txt_units)] + [(2, 0)]
 
     barrier = pltpu.get_barrier_semaphore()
-    partners = [peer_of(me, axis, d) for axis in "cxyz" for d in range(1, AXES[axis][0])]
-    for dev in partners:
-        pl.semaphore_signal(barrier, inc=1, device_id=(dev,), device_id_type=MESH_ID)
-    pl.semaphore_wait(barrier, len(partners))
-
-    counter = [0]
+    for axis in "cxyuv":
+        pl.semaphore_signal(barrier, inc=1, device_id=(peers[axis],), device_id_type=MESH_ID)
+    pl.semaphore_wait(barrier, 5)
+
+    base = [0] * n
+    home = [0] * n
+    pending = [None] * n
     started = []
 
-    def send(src, dst, dev):
-        k = counter[0]
-        counter[0] += 1
-        copy = pltpu.make_async_remote_copy(
+    def send(i, stage, src, dst):
+        k = len(started)
+        pending[i] = pltpu.make_async_remote_copy(
             src_ref=src, dst_ref=dst, send_sem=send_sem.at[k], recv_sem=recv_sem.at[k],
-            device_id=(dev,), device_id_type=MESH_ID)
-        copy.start()
-        started.append(copy)
-        return copy
-
-    offs = [0] * n
-    pending = [None] * n
+            device_id=(peers[orders[i][stage]],), device_id_type=MESH_ID)
+        pending[i].start()
+        started.append(pending[i])
 
     def scatter(i, stage):
-        slab = slabs[i]
-        axis = slab.order[stage]
-        size = AXES[axis][0]
-        piece = slab.piece(stage)
-        here = coordinate(me, axis)
-        copies = []
-        for d in range(1, size):
-            there = lax.rem(here + d, size)
-            if stage == 0:
-                src = slab.src.at[rows_at(slab.row0 + there * piece, piece)]
-            else:
-                src = held[i].at[rows_at(offs[i] + there * piece, piece)]
-            copies.append(send(src, land[4 * i + stage].at[d - 1], peer_of(me, axis, d)))
-        pending[i] = copies
+        size = UNIT >> (stage + 1)
+        other = (1 - bits[orders[i][stage]]) * size
+        array, row0 = place[i]
+        src = ins[array].at[rows_at(row0 + other, size)] if stage == 0 else held[i].at[rows_at(base[i] + other, size)]
+        send(i, stage, src, land[5 * i + stage])
+
+    def spread(i, stage):
+        array, row0 = place[i]
+        view = outs[array].at[rows_at(row0 + home[i], UNIT >> (stage + 1))]
+        send(i, stage, view, view)
 
     def absorb(i, stage):
-        slab = slabs[i]
-        axis = slab.order[stage]
-        piece = slab.piece(stage)
-        here = coordinate(me, axis)
-        for copy in pending[i]:
-            copy.wait_recv()
-        base = offs[i] + here * piece
-        step = min(piece, 32)
+        pending[i].wait_recv()
+        size = UNIT >> (stage + 1)
+        array, row0 = place[i]
+        mine = bits[orders[i][stage]] * size
+        home[i] = home[i] + mine
+        step = min(size, 32)
 
         def add(k, _):
             at = k * step
+            part = land[5 * i + stage][rows_at(at, step), :]
             if stage == 0:
-                total = slab.src[rows_at(slab.row0 + base + at, step), :]
+                held[i][rows_at(at, step), :] = ins[array][rows_at(row0 + mine + at, step), :] + part
+            elif stage == 4:
+                outs[array][rows_at(row0 + home[i] + at, step), :] = held[i][rows_at(base[i] + mine + at, step), :] + part
             else:
-                total = held[i][rows_at(base + at, step), :]
-            for d in range(AXES[axis][0] - 1):
-                total = total + land[4 * i + stage][d, rows_at(at, step), :]
-            if stage == 0:
-                held[i][rows_at(at, step), :] = total
-            elif stage == 3:
-                slab.dst[rows_at(slab.row0 + home[i] + at, step), :] = total
-            else:
-                held[i][rows_at(base + at, step), :] = total
+                held[i][rows_at(base[i] + mine + at, step), :] += part
             return 0
 
-        if stage == 0:
-            home[i] = here * piece
-        else:
-            home[i] = home[i] + here * piece
-        lax.fori_loop(0, piece // step, add, 0)
-        offs[i] = 0 if stage == 0 else base
-
-    home = [0] * n
+        lax.fori_loop(0, size // step, add, 0)
+        base[i] = 0 if stage == 0 else base[i] + mine
 
     for i in range(n):
         scatter(i, 0)
-    for stage in range(4):
-        for i in range(n):
+    for code in steps:
+        i, stage = divmod(code, 10)
+        if stage < 5:
             absorb(i, stage)
-            if stage < 3:
+            if stage < 4:
                 scatter(i, stage + 1)
             else:
-                spread(i, 3, slabs, home, me, send, pending)
-    for stage in (2, 1, 0):
-        for i in range(n):
-            for copy in pending[i]:
-                copy.wait_recv()
-            here = coordinate(me, slabs[i].order[stage + 1])
-            home[i] = home[i] - here * slabs[i].piece(stage + 1)
-            spread(i, stage, slabs, home, me, send, pending)
-    for i in range(n):
-        for copy in pending[i]:
-            copy.wait_recv()
+                spread(i, 4)
+        else:
+            pending[i].wait_recv()
+            left = 9 - stage
+            home[i] = home[i] - bits[orders[i][left]] * (UNIT >> (left + 1))
+            if left > 0:
+                spread(i, left - 1)
     for copy in started:
         copy.wait_send()
 
 
-def spread(i, stage, slabs, home, me, send, pending):
-    slab = slabs[i]
-    axis = slab.order[stage]
-    piece = slab.piece(stage)
-    view = slab.dst.at[rows_at(slab.row0 + home[i], piece)]
-    pending[i] = [send(view, view, peer_of(me, axis, d)) for d in range(1, AXES[axis][0])]
-
-
-def sum_over_devices(dw_img, dw_txt, small, sub=2):
-    plan = sum_plan(dw_img.shape[0], dw_txt.shape[0], sub)
+def sum_over_devices(dw_img, dw_txt, small):
     arrays = [dw_img, dw_txt, small]
-    held, land = [], []
-    copies = 0
-    for a, _, rows, order in plan:
-        width = arrays[a].shape[1]
-        slab = Slab(None, None, 0, rows, order)
-        held.append(pltpu.VMEM((slab.piece(0), width), jnp.float32))
-        for stage in range(4):
-            others = AXES[order[stage]][0] - 1
-            land.append(pltpu.VMEM((others, slab.piece(stage), width), jnp.float32))
-            copies += 2 * others
+    orders = SUM_ORDERS + (SUM_ORDERS[-1],)
+    widths = [dw_img.shape[1]] * len(SUM_ORDERS) + [small.shape[1]]
+    held = [pltpu.VMEM((UNIT // 2, width), jnp.float32) for width in widths]
+    land = [pltpu.VMEM((UNIT >> (stage + 1), width), jnp.float32) for width in widths for stage in range(5)]
+    copies = 10 * len(orders)
     return pl.pallas_call(
-        functools.partial(sum_kernel, plan),
+        functools.partial(sum_kernel, orders, SUM_STEPS),
         out_shape=[jax.ShapeDtypeStruct(a.shape, jnp.float32) for a in arrays],
         in_specs=[pl.BlockSpec(memory_space=pltpu.VMEM)] * 3,
         out_specs=[pl.BlockSpec(memory_space=pltpu.VMEM)] * 3,

time: 365 us -> 342 us (0.937)
  Pallas kernels: 319 us -> 296 us
    pallas_call x1, Pallas kernels: 126 us -> 103 us  [sum_over_devices(): pl.pallas_call(functools.partial(sum_kernel, orders, SUM_STEPS), out_shap...]
where the time goes in v3:
time: 342 us
  Pallas kernels  296 us (87%)
  matrix products  15.7 us (5%)
  local copies, waits for them, and re-layouts  14.9 us (4%)
  other arithmetic  9.67 us (3%)
  between operations  5.15 us (2%)
    pallas_call x1, Pallas kernels, cross_pass(): pl.pallas_call(cross_kernel, out_shape=[jax.ShapeDtypeStruct((rows, emb),...  193 us
    pallas_call x1, Pallas kernels, sum_over_devices(): pl.pallas_call(functools.partial(sum_kernel, orders, SUM_STEPS), out_shap...  103 us
    unnamed x20, local copies, waits for them, and re-layouts  12.2 us
    dot_general x2, matrix products, weight_grad(): lax.dot_general(feat_rows, raw_grad.astype(jnp.bfloat16), CONTRACT_ROWS,...  8.4 us
    dot_general x2, matrix products, embed_rows(): raw_emb = jnp.dot(feat_rows, weights, preferred_element_type=jnp.float32)  7.27 us

profile of v3, /device:TPU:0, one launch (start us, length us, event | category | flops | bytes accessed | tf_op | source)
XLA Modules:
  0.0 341.6 jit_solution(5761542952490998650)
XLA Ops:
  2.0 0.6 pad_maximum_fusion.1.scal_ref
  2.6 0.7 fusion.10
  3.3 1.9 fusion.9.txt_in
  5.2 5.2 %multiply_reduce_fusion.3 = (f32[512]{0:T(512)S(1)}, f32[512,1024]{1,0:T(8,128)S(1)}) fusion(bf16[512,2048]{1,0:T(8,128)(2,1)} %param.7, bf16[2048,1024]{1,0:T(8,128)(2,1)} %param.9), kind=kOutput, calls=%fused_computation.8 | convolution fusion | flops 2148531712 | bytes 8390656 | tf_op jit(solution)/shard_map/dot_general | solution.py:18
  10.4 0.2 multiply_convert_fusion.2
  10.6 1.1 fusion.1.img_in
  11.7 0.4 copy-done.1
  12.1 0.9 copy-done.6
  13.0 2.0 multiply_reduce_fusion.1
  15.0 193.3 %shard_map.115 = (f32[512,1024]{1,0:T(8,128)}, f32[512,1024]{1,0:T(8,128)}, f32[4,8,256]{2,1,0:T(8,128)}) custom-call(f32[2]{0:T(128)} %pad_maximum_fusion.1.scal_ref, bf16[528,1024]{1,0:T(8,128)(2,1)} %fusion.1.img_in, bf16[528,512]{1,0:T(8,128)(2,1)} %fusion.9.txt_in, bf16[512,1024]{1,0:T(8,128)(2,1)} %w_ref.1), custom_call_target="tpu_custom_call" | custom-call | tf_op jit(solution)/shard_map/pallas_call | solution.py:425
  208.3 0.9 reduce_sum.49
  209.2 0.1 slice_bitcast_fusion
  209.3 0.6 fusion.13
  211.2 0.1 copy.17
  211.3 4.3 %multiply_reduce_fusion = (f32[512]{0:T(512)S(1)}, f32[512]{0:T(512)S(1)}) fusion(f32[512,1024]{1,0:T(8,128)} %get-tuple-element.27, f32[512,1024]{1,0:T(8,128)} %get-tuple-element.12, f32[512]{0:T(512)S(1)} %rsqrt.17, f32[]{:T(128)S(6)} %div.22, f32[512,1024]{1,0:T(8,128)} %get-tuple-element.11, f32[512,1024]{1,0:T(8,128)} %copy-done.1, f32[512]{0:T(512)S(1)} %rsqrt.16), kind=kLoop, calls=%fused_computation.4 | loop fusion | flops 4193280 | bytes 8396804 | tf_op jit(solution)/shard_map/reduce_sum | solution.py:25
  215.6 0.4 copy-done.3
  216.0 2.4 convolution_bitcast_fusion.1.refs_1_
  218.4 0.7 pad.14.refs_2_
  219.1 0.6 copy-done.8
  219.7 6.0 %convolution_bitcast_fusion.refs_0_ = f32[2048,1024]{1,0:T(8,128)} fusion(bf16[512,2048]{1,0:T(8,128)(2,1)S(1)} %copy-done.8, f32[512,1024]{1,0:T(8,128)S(1)} %copy-done.4, f32[512,1024]{1,0:T(8,128)S(1)} %copy-done.2, f32[512]{0:T(512)S(1)} %get-tuple-element.29, f32[]{:T(128)S(6)} %div.22, f32[512]{0:T(512)S(1)} %rsqrt.16), kind=kOutput, calls=%fused_computation | convolution fusion | flops 2150629376 | bytes 14684164 | tf_op jit(solution)/shard_map/dot_general | solution.py:26
  225.7 102.9 %shard_map.116 = (f32[2048,1024]{1,0:T(8,128)}, f32[512,1024]{1,0:T(8,128)}, f32[256,128]{1,0:T(8,128)}) custom-call(f32[2048,1024]{1,0:T(8,128)} %convolution_bitcast_fusion.refs_0_, f32[512,1024]{1,0:T(8,128)} %convolution_bitcast_fusion.1.refs_1_, f32[256,128]{1,0:T(8,128)} %pad.14.refs_2_), custom_call_target="tpu_custom_call" | custom-call | tf_op jit(solution)/shard_map/pallas_call | solution.py:166
  328.6 1.3 fusion.12
  330.6 8.6 %copy.24 = f32[2048,1024]{1,0:T(8,128)} copy(f32[2048,1024]{1,0:T(8,128)} %get-tuple-element.38) | data formatting | bytes 16777216
  339.2 1.3 copy.25
  (21 shorter events, 0.1 us)
Async XLA Ops:
  10.4 1.7 copy-start.1
  10.4 1.7 copy-start.5
  10.4 2.5 copy-start.6
  211.3 4.3 %copy-start = (f32[512,1024]{1,0:T(8,128)S(1)}, f32[512,1024]{1,0:T(8,128)}, u32[]{:S(2)}) copy-start(f32[512,1024]{1,0:T(8,128)} %get-tuple-element.27) | copy-start | bytes 6291460
  211.3 4.7 %copy-start.3 = (f32[512,1024]{1,0:T(8,128)S(1)}, f32[512,1024]{1,0:T(8,128)}, u32[]{:S(2)}) copy-start(f32[512,1024]{1,0:T(8,128)} %get-tuple-element.12) | copy-start | bytes 6291460
  216.0 3.0 copy-start.2
  216.0 3.0 copy-start.4
  216.0 3.7 %copy-start.8 = (bf16[512,2048]{1,0:T(8,128)(2,1)S(1)}, bf16[512,2048]{1,0:T(8,128)(2,1)}, u32[]{:S(2)}) copy-start(bf16[512,2048]{1,0:T(8,128)(2,1)} %param.7) | copy-start | bytes 6291460
  330.6 8.6 %copy-start.7 = (f32[512,1024]{1,0:T(8,128)S(1)}, f32[512,1024]{1,0:T(8,128)}, u32[]{:S(2)}) copy-start(f32[512,1024]{1,0:T(8,128)} %get-tuple-element.39) | copy-start | bytes 6291460

commit v4 on v3

--- a/solution.py
+++ b/solution.py
@@ -21,9 +21,9 @@
     return unit_emb, inv_norm, unit_emb.astype(jnp.bfloat16)
 
 
-def weight_grad(feat_rows, unit_emb, inv_norm, grad_emb):
-    raw_grad = inv_norm * (grad_emb - unit_emb * jnp.sum(unit_emb * grad_emb, axis=1, keepdims=True))
-    return lax.dot_general(feat_rows, raw_grad.astype(jnp.bfloat16), CONTRACT_ROWS, preferred_element_type=jnp.float32)
+def raw_grad(unit_emb, inv_norm, grad_emb):
+    grad = inv_norm * (grad_emb - unit_emb * jnp.sum(unit_emb * grad_emb, axis=1, keepdims=True))
+    return grad.astype(jnp.bfloat16)
 
 
 def log1p_sum(expo):
@@ -72,16 +72,17 @@
 
 
 def sum_kernel(orders, steps, *refs):
-    ins, outs = refs[:3], refs[3:6]
     n = len(orders)
-    held = refs[6:6 + n]
-    land = refs[6 + n:6 + 6 * n]
-    send_sem, recv_sem = refs[6 + 6 * n:]
+    feats, grads, outs = refs[0:2], refs[2:4], refs[5:8]
+    ins = (refs[8], refs[9], refs[4])
+    held = refs[10:10 + n]
+    land = refs[10 + n:10 + 6 * n]
+    send_sem, recv_sem = refs[10 + 6 * n:]
     me = lax.axis_index("data")
     bits = {axis: coordinate(me, axis) for axis in "cxyuv"}
     peers = {axis: peer_of(me, axis) for axis in "cxyuv"}
-    img_units = ins[0].shape[0] // UNIT
-    txt_units = ins[1].shape[0] // UNIT
+    img_units = outs[0].shape[0] // UNIT
+    txt_units = outs[1].shape[0] // UNIT
     place = [(0, u * UNIT) for u in range(img_units)] + [(1, u * UNIT) for u in range(txt_units)] + [(2, 0)]
 
     barrier = pltpu.get_barrier_semaphore()
@@ -137,6 +138,11 @@
         base[i] = 0 if stage == 0 else base[i] + mine
 
     for i in range(n):
+        array, row0 = place[i]
+        if array < 2:
+            ins[array][pl.ds(row0, UNIT), :] = lax.dot_general(
+                feats[array][:, pl.ds(row0, UNIT)], grads[array][...], CONTRACT_ROWS,
+                preferred_element_type=jnp.float32)
         scatter(i, 0)
     for code in steps:
         i, stage = divmod(code, 10)
@@ -156,22 +162,23 @@
         copy.wait_send()
 
 
-def sum_over_devices(dw_img, dw_txt, small):
-    arrays = [dw_img, dw_txt, small]
+def sum_over_devices(feats, grads, small):
+    emb = grads[0].shape[1]
+    shapes = [(feat.shape[1], emb) for feat in feats] + [small.shape]
     orders = SUM_ORDERS + (SUM_ORDERS[-1],)
-    widths = [dw_img.shape[1]] * len(SUM_ORDERS) + [small.shape[1]]
+    widths = [emb] * len(SUM_ORDERS) + [small.shape[1]]
     held = [pltpu.VMEM((UNIT // 2, width), jnp.float32) for width in widths]
     land = [pltpu.VMEM((UNIT >> (stage + 1), width), jnp.float32) for width in widths for stage in range(5)]
     copies = 10 * len(orders)
     return pl.pallas_call(
         functools.partial(sum_kernel, orders, SUM_STEPS),
-        out_shape=[jax.ShapeDtypeStruct(a.shape, jnp.float32) for a in arrays],
-        in_specs=[pl.BlockSpec(memory_space=pltpu.VMEM)] * 3,
+        out_shape=[jax.ShapeDtypeStruct(shape, jnp.float32) for shape in shapes],
+        in_specs=[pl.BlockSpec(memory_space=pltpu.VMEM)] * 5,
         out_specs=[pl.BlockSpec(memory_space=pltpu.VMEM)] * 3,
-        scratch_shapes=held + land + [pltpu.SemaphoreType.DMA((copies,)), pltpu.SemaphoreType.DMA((copies,))],
+        scratch_shapes=[pltpu.VMEM(shape, jnp.float32) for shape in shapes[:2]] + held + land + [pltpu.SemaphoreType.DMA((copies,)), pltpu.SemaphoreType.DMA((copies,))],
         compiler_params=pltpu.CompilerParams(
             collective_id=1, has_side_effects=True, vmem_limit_bytes=60 * 1024 * 1024),
-    )(*arrays)
+    )(*feats, *grads, small)
 
 
 ID_ROWS = 16
@@ -453,12 +460,12 @@
         unit_txt, inv_txt, _ = embed_rows(feat_txt, w_txt)
         acc_img, acc_txt, sums = cross_pass(scalars, with_ids(emb_img, pair_ids), with_ids(feat_txt, pair_ids), w_txt)
         out_scale = temp_scale / total_rows
-        dw_img = weight_grad(feat_img, unit_img, inv_img, out_scale * acc_img)
-        dw_txt = weight_grad(feat_txt, unit_txt, inv_txt, out_scale * acc_txt)
+        grad_img = raw_grad(unit_img, inv_img, out_scale * acc_img)
+        grad_txt = raw_grad(unit_txt, inv_txt, out_scale * acc_txt)
         sums = jnp.sum(sums, axis=(1, 2))
         small = jnp.stack([LN2 * sums[0] + sums[1], sums[2], sums[3]]) / total_rows
         small = jnp.pad(small[:, None], ((0, 253), (0, 127)))
-        dw_img, dw_txt, small = sum_over_devices(dw_img, dw_txt, small)
+        dw_img, dw_txt, small = sum_over_devices((feat_img, feat_txt), (grad_img, grad_txt), small)
         return small[0, 0], temp_scale * small[1, 0], small[2, 0], dw_img, dw_txt
 
     return jax.shard_map(

time: 342 us -> 333 us (0.974)
  matrix products: 15.7 us -> 7.27 us
    dot_general x2 -> x0, matrix products: 8.4 us -> none  [weight_grad(): lax.dot_general(feat_rows, raw_grad.astype(jnp.bfloat16), CONTRACT_ROWS,...]
    unnamed x20 -> x18, local copies, waits for them, and re-layouts: 12.2 us -> 13.7 us
where the time goes in v4:
time: 333 us; the launch traced here: 332 us
  Pallas kernels  293 us (88%)
  local copies, waits for them, and re-layouts  16.4 us (5%)
  other arithmetic  10.7 us (3%)
  matrix products  7.27 us (2%)
  between operations  5.14 us (2%)
    pallas_call x1, Pallas kernels, cross_pass(): pl.pallas_call(cross_kernel, out_shape=[jax.ShapeDtypeStruct((rows, emb),...  193 us
    pallas_call x1, Pallas kernels, sum_over_devices(): pl.pallas_call(functools.partial(sum_kernel, orders, SUM_STEPS), out_shap...  99.6 us
    unnamed x18, local copies, waits for them, and re-layouts  13.7 us
    dot_general x2, matrix products, embed_rows(): raw_emb = jnp.dot(feat_rows, weights, preferred_element_type=jnp.float32)  7.27 us

profile of v4, /device:TPU:0, one launch (start us, length us, event | category | flops | bytes accessed | tf_op | source)
XLA Modules:
  0.0 332.4 jit_solution(11460355850549310323)
XLA Ops:
  2.0 0.6 pad_maximum_fusion.1.scal_ref
  2.6 0.7 fusion.4
  3.3 1.9 fusion.3.txt_in
  5.2 5.2 %multiply_reduce_fusion.3 = (f32[512]{0:T(512)S(1)}, f32[512,1024]{1,0:T(8,128)S(1)}) fusion(bf16[512,2048]{1,0:T(8,128)(2,1)} %refs_0_.1, bf16[2048,1024]{1,0:T(8,128)(2,1)} %param.9), kind=kOutput, calls=%fused_computation.7 | convolution fusion | flops 2148531712 | bytes 8390656 | tf_op jit(solution)/shard_map/dot_general | solution.py:18
  10.5 0.2 multiply_convert_fusion.2
  10.6 1.1 fusion.1.img_in
  11.7 0.4 copy-done
  12.1 0.9 copy-done.6
  13.0 2.0 multiply_reduce_fusion.1
  15.0 193.3 %shard_map.115 = (f32[512,1024]{1,0:T(8,128)}, f32[512,1024]{1,0:T(8,128)}, f32[4,8,256]{2,1,0:T(8,128)}) custom-call(f32[2]{0:T(128)} %pad_maximum_fusion.1.scal_ref, bf16[528,1024]{1,0:T(8,128)(2,1)} %fusion.1.img_in, bf16[528,512]{1,0:T(8,128)(2,1)} %fusion.3.txt_in, bf16[512,1024]{1,0:T(8,128)(2,1)} %w_ref.1), custom_call_target="tpu_custom_call" | custom-call | tf_op jit(solution)/shard_map/pallas_call | solution.py:432
  208.3 0.9 reduce_sum.49
  209.3 0.6 fusion.7
  211.2 0.1 copy.13
  211.3 2.8 multiply_reduce_fusion.2
  214.2 0.6 copy-done.4
  214.8 0.4 multiply_reduce_fusion
  215.3 1.2 copy-done.1
  216.4 0.6 copy-done.3
  217.1 2.1 multiply_convert_fusion
  219.2 0.7 pad.14.refs_4_
  219.8 99.6 %shard_map.116 = (f32[2048,1024]{1,0:T(8,128)}, f32[512,1024]{1,0:T(8,128)}, f32[256,128]{1,0:T(8,128)}) custom-call(bf16[512,2048]{1,0:T(8,128)(2,1)} %refs_0_.1, bf16[512,512]{1,0:T(8,128)(2,1)} %refs_1_.1, bf16[512,1024]{1,0:T(8,128)(2,1)} %get-tuple-element.29.refs_2_, bf16[512,1024]{1,0:T(8,128)(2,1)} %get-tuple-element.28.refs_3_, f32[256,128]{1,0:T(8,128)} %pad.14.refs_4_), custom_call_target="tpu_custom_call" | custom-call | tf_op jit(solution)/shard_map/pallas_call | solution.py:173
  319.4 1.3 fusion.6
  321.4 8.6 %copy.18 = f32[2048,1024]{1,0:T(8,128)} copy(f32[2048,1024]{1,0:T(8,128)} %get-tuple-element.38) | data formatting | bytes 16777216
  330.0 1.3 copy.19
  (19 shorter events, 0.3 us)
Async XLA Ops:
  10.4 1.7 copy-start
  10.4 1.7 copy-start.5
  10.4 2.5 copy-start.6
  211.3 2.9 copy-start.2
  211.3 3.5 %copy-start.4 = (f32[512,1024]{1,0:T(8,128)S(1)}, f32[512,1024]{1,0:T(8,128)}, u32[]{:S(2)}) copy-start(f32[512,1024]{1,0:T(8,128)} %get-tuple-element.12) | copy-start | bytes 6291460
  214.8 1.6 copy-start.1
  214.8 2.2 copy-start.3
  321.4 8.6 %copy-start.7 = (f32[512,1024]{1,0:T(8,128)S(1)}, f32[512,1024]{1,0:T(8,128)}, u32[]{:S(2)}) copy-start(f32[512,1024]{1,0:T(8,128)} %get-tuple-element.39) | copy-start | bytes 6291460
